TPU v7x, 32 devices: a whole 2x2x4 slice. The times are simulated.
32 devices in a mesh: dp: 8 (over z, x), expert: 4 (over y, core).
Axes of the slice: x: 2, y: 2, z: 4, core: 2. Of those that a mesh axis runs over, the one named last changes fastest.
Arguments:
- tokens: bfloat16 [4096, 2048], P(('dp', 'expert')), may hold values from -6 to 6
- expert_ids: int32 [4096, 8], P(('dp', 'expert')), may hold values from 0 to 15, all different within a row
- route_probs: float32 [4096, 8], P(('dp', 'expert')), may hold values from 0.05 to 1
- shard_limit: int32 [32, 16], P(('dp', 'expert')), may hold values from 32 to 64
- gate_proj: bfloat16 [32, 2048, 384], P(('dp', 'expert')), may hold values from -0.125 to 0.125
- up_proj: bfloat16 [32, 2048, 384], P(('dp', 'expert')), may hold values from -0.125 to 0.125
- down_proj: bfloat16 [32, 384, 2048], P(('dp', 'expert')), may hold values from -0.21875 to 0.21875
Outputs:
- mixed_out: bfloat16 [4096, 2048], P(('dp', 'expert'))
Inputs may be any that keep to these rules, and one draw needn't show every extreme that they name: `expert_ids`: each row names 8 different experts.
All inputs are finite; a program needn't handle non-finite values.
Results may differ from a plain program's by a relative error of at most 0.0095.
Values may be sent and summed in bfloat16 or wider, within the bound.
A program may use at most 64 MiB of HBM per device.

v0:
```python
import jax
import jax.numpy as jnp
from jax import lax
from jax.sharding import PartitionSpec as P


def partner_2(block, axis, distance):
    count = lax.axis_size(axis)
    route = []
    for low in range(count):
        high = low | 1 << distance
        if high != low and high < count:
            route += [(low, high), (high, low)]
    return lax.ppermute(block, axis, route)


def half_ffn(rows_in, gate_half, up_half, down_half):
    gate_val = jnp.dot(rows_in, gate_half, preferred_element_type=jnp.float32)
    up_val = jnp.dot(rows_in, up_half, preferred_element_type=jnp.float32)
    hidden = (jax.nn.silu(gate_val) * up_val).astype(jnp.bfloat16)
    return jnp.dot(hidden, down_half, preferred_element_type=jnp.float32).astype(jnp.bfloat16)


def on_device(tokens, expert_ids, route_probs, shard_limit, gate_proj, up_proj, down_proj):
    tok_rows, feature_width = tokens.shape
    top_count = expert_ids.shape[1]
    experts = shard_limit.shape[1]
    dp_size = lax.axis_size("dp")
    col_size = lax.axis_size("expert")
    capacity = tok_rows * top_count // experts
    col_cap = dp_size * capacity // 2
    flat_ids = expert_ids.reshape(-1)
    onehot = (flat_ids[:, None] == jnp.arange(experts, dtype=jnp.int32)[None, :]).astype(jnp.int32)
    before = jnp.cumsum(onehot, axis=0) - onehot
    slot_rank = jnp.sum(before * onehot, axis=1)
    expert_count = jnp.sum(onehot, axis=0)
    limits = shard_limit[0]
    kept_count = jnp.minimum(expert_count, limits)
    count_table = lax.all_gather(kept_count[None, :], "dp", axis=0, tiled=True)
    earlier = (jnp.arange(dp_size, dtype=jnp.int32) < lax.axis_index("dp")).astype(jnp.int32)
    offset = jnp.sum(count_table * earlier[:, None], axis=0)
    limit_each = jnp.sum(onehot * limits[None, :], axis=1)
    offset_each = jnp.sum(onehot * offset[None, :], axis=1)
    kept_mask = (slot_rank < limit_each) & (offset_each + slot_rank < col_cap)
    slots_total = experts * capacity
    position = jnp.where(kept_mask, flat_ids * capacity + slot_rank, slots_total)
    source = jnp.repeat(tokens, top_count, axis=0)
    sendbuf = (
        jnp.zeros((slots_total, feature_width), jnp.bfloat16).at[position].set(source, mode="drop")
    )
    sendbuf = sendbuf.reshape(dp_size, col_size, capacity // 2, feature_width)
    arrived = lax.all_to_all(
        lax.all_to_all(sendbuf, "dp", split_axis=0, concat_axis=2, tiled=True),
        "expert",
        split_axis=1,
        concat_axis=1,
        tiled=True,
    )
    held_rows = arrived.reshape(-1, feature_width)
    held_count = held_rows.shape[0]
    gate_half = gate_proj[0]
    up_half = up_proj[0]
    down_half = down_proj[0]
    partner = partner_2(held_rows, "expert", 0)
    stacked = jnp.concatenate([held_rows, partner], axis=0)
    partials = half_ffn(stacked, gate_half, up_half, down_half)
    returned_part = partner_2(partials[held_count:], "expert", 0)
    merged = (partials[:held_count].astype(jnp.float32) + returned_part.astype(jnp.float32)).astype(
        jnp.bfloat16
    )
    returned = lax.all_to_all(
        lax.all_to_all(
            merged.reshape(1, col_size, -1, feature_width),
            "dp",
            split_axis=2,
            concat_axis=0,
            tiled=True,
        ),
        "expert",
        split_axis=1,
        concat_axis=1,
        tiled=True,
    )
    results = returned.reshape(slots_total, feature_width)
    fetched = results[jnp.minimum(position, slots_total - 1)].astype(jnp.float32)
    weight = route_probs.reshape(-1) * kept_mask.astype(jnp.float32)
    mixed_out = jnp.sum(
        (weight[:, None] * fetched).reshape(tok_rows, top_count, feature_width), axis=1
    )
    return mixed_out.astype(jnp.bfloat16)


def solution(mesh):
    in_specs = (
        P(("dp", "expert"), None),
        P(("dp", "expert"), None),
        P(("dp", "expert"), None),
        P(("dp", "expert"), None),
        P(("dp", "expert"), None, None),
        P(("dp", "expert"), None, None),
        P(("dp", "expert"), None, None),
    )
    out_specs = P(("dp", "expert"), None)
    return jax.shard_map(
        on_device, mesh=mesh, in_specs=in_specs, out_specs=out_specs, check_vma=False
    )
```

profile of v0, /device:TPU:0, one launch (start us, length us, event | category | flops | bytes accessed | tf_op | source)
XLA Modules:
  0.0 397.7 jit_solution(4428057874876213967)
XLA Ops:
  0.0 0.0 copy-start
  0.0 0.9 copy.27
  0.9 0.1 eq.29
  1.0 0.1 eq.25
  1.1 0.7 broadcast_multiply_fusion
  1.8 4.5 %reduce-window.6 = s32[16,8,128]{2,1,0:T(8,128)S(1)} reduce-window(s32[16,8,128]{2,1,0:T(8,128)S(1)} %fusion.13, s32[]{:T(128)} %constant.10.clone.1), window={size=1x1x128 pad=0_0x0_0x127_0}, to_apply=%region_0.0 | reduce-window | flops 2080768 | bytes 131076 | tf_op jit(solution)/shard_map/reduce-window
  6.3 0.1 slice.18
  6.4 0.1 copy.29
  6.6 0.1 copy.30
  6.6 0.1 broadcast_add_fusion
  6.7 0.1 convert_reduce_fusion
  6.9 0.7 fusion.15
  7.5 22.3 %all-gather = s32[8,1,16]{2,1,0:T(1,128)S(1)} all-gather(s32[1,1,16]{2,1,0:T(1,128)S(1)} %fusion.15), channel_id=1, replica_groups=mesh['dp'=8,'expert'=4] {'dp'}, dimensions={0}, use_global_device_ids=true | all-gather | bytes 576 | tf_op jit(solution)/shard_map/all_gather | solution.py:39
  29.8 0.1 copy.32
  29.9 0.1 mul.80
  30.0 0.1 multiply_reduce_fusion
  30.1 0.8 select_reduce_fusion
  30.9 9.5 %scatter_custom_fusion = bf16[1024,2048]{1,0:T(8,128)(2,1)} fusion(s32[1024]{0:T(1024)S(1)} %bitcast.71, bf16[128,2048]{1,0:T(8,128)(2,1)} %param.7, bf16[]{:T(256)} %constant.27.clone.1), kind=kCustom, calls=%fused_computation.9 | custom fusion | bytes 4718594 | tf_op jit(solution)/shard_map/scatter | solution.py:49
  40.3 93.3 %all_to_all.46 = bf16[8,4,32,2048]{3,2,1,0:T(8,128)(2,1)S(1)} all-to-all(bf16[8,4,32,2048]{3,2,1,0:T(8,128)(2,1)} %bitcast.57), channel_id=1, replica_groups=mesh['dp'=8,'expert'=4] {'dp'}, dimensions={0} | all-to-all | bytes 8388608 | tf_op jit(solution)/shard_map/all_to_all | solution.py:53
  133.6 0.6 copy.33
  134.2 0.0 copy-start.3
  134.2 50.9 %all_to_all.47 = bf16[1,4,256,2048]{3,2,0,1:T(8,128)(2,1)S(1)} all-to-all(bf16[1,4,256,2048]{3,2,0,1:T(8,128)(2,1)S(1)} %bitcast.59), channel_id=1, replica_groups=mesh['dp'=8,'expert'=4] {'expert'}, dimensions={1} | all-to-all | bytes 8388608 | tf_op jit(solution)/shard_map/all_to_all | solution.py:52
  185.1 0.0 copy-start.4
  185.1 0.0 collective-permute-start
  185.1 7.2 %collective-permute-done = bf16[1024,2048]{1,0:T(8,128)(2,1)S(1)} collective-permute-done((bf16[1024,2048]{1,0:T(8,128)(2,1)S(1)}, bf16[1024,2048]{1,0:T(8,128)(2,1)S(1)}, u32[]{:S(2)}, u32[]{:S(2)}) %collective-permute-start) | collective-permute-done | bytes 4194336 | tf_op jit(solution)/shard_map/ppermute | solution.py:14
  192.2 0.0 copy-done.3
  192.2 4.6 %fusion.2 = f32[2048,384]{1,0:T(8,128)S(1)} fusion(bf16[1024,2048]{1,0:T(8,128)(2,1)S(1)} %collective-permute-done, bf16[1024,2048]{1,0:T(8,128)(2,1)S(1)} %bitcast.62, bf16[1,2048,384]{2,1,0:T(8,128)(2,1)S(1)} %copy-done.3), kind=kOutput, calls=%fused_computation.8 | convolution fusion | flops 3238002688 | bytes 13107200 | tf_op jit(solution)/shard_map/dot_general | solution.py:18
  196.9 0.0 copy-done.4
  196.9 4.7 %fusion.1 = f32[2048,384]{1,0:T(8,128)S(1)} fusion(bf16[1024,2048]{1,0:T(8,128)(2,1)S(1)} %collective-permute-done, bf16[1024,2048]{1,0:T(8,128)(2,1)S(1)} %bitcast.63, bf16[1,2048,384]{2,1,0:T(8,128)(2,1)S(1)} %copy-done.4), kind=kOutput, calls=%fused_computation.7 | convolution fusion | flops 3238002688 | bytes 13107200 | tf_op jit(solution)/shard_map/dot_general | solution.py:19
  201.6 0.0 copy-done
  201.6 5.0 %convolution_convert_fusion = bf16[2048,2048]{1,0:T(8,128)(2,1)S(1)} fusion(f32[2048,384]{1,0:T(8,128)S(1)} %fusion.1, f32[2048,384]{1,0:T(8,128)S(1)} %fusion.2, bf16[1,384,2048]{2,1,0:T(8,128)(2,1)S(1)} %copy-done), kind=kOutput, calls=%fused_computation.6 | convolution fusion | flops 3230138368 | bytes 16252928 | tf_op jit(solution)/shard_map/dot_general | solution.py:21
  206.6 0.3 slice.21
  206.9 0.2 collective-permute-start.1
  207.1 7.0 %collective-permute-done.1 = bf16[1024,2048]{1,0:T(8,128)(2,1)S(1)} collective-permute-done((bf16[1024,2048]{1,0:T(8,128)(2,1)S(1)}, bf16[1024,2048]{1,0:T(8,128)(2,1)S(1)}, u32[]{:S(2)}, u32[]{:S(2)}) %collective-permute-start.1) | collective-permute-done | bytes 4194336 | tf_op jit(solution)/shard_map/ppermute | solution.py:14
  214.1 2.3 add_convert_fusion
  216.4 3.2 copy.35
  219.7 96.8 %all_to_all.48 = bf16[1,4,256,2048]{3,1,0,2:T(4,128)(2,1)S(1)} all-to-all(bf16[1,4,256,2048]{3,1,0,2:T(4,128)(2,1)S(1)} %copy.35), channel_id=1, replica_groups=mesh['dp'=8,'expert'=4] {'dp'}, dimensions={2} | all-to-all | bytes 8388608 | tf_op jit(solution)/shard_map/all_to_all | solution.py:72
  316.5 4.3 %copy.41 = bf16[1,4,8,32,2048]{4,3,2,1,0:T(8,128)(2,1)} copy(bf16[1,4,8,32,2048]{4,1,3,2,0:T(4,128)(2,1)S(1)} %bitcast.60) | data formatting | bytes 8388608 | tf_op jit(solution)/shard_map/all_to_all | solution.py:72
  320.7 0.0 copy-start.2
  320.7 5.2 %all-to-all-start.3 = ((bf16[8,4,32,2048]{3,2,0,1:T(8,128)(2,1)}), bf16[8,4,32,2048]{3,2,0,1:T(8,128)(2,1)}, u32[]{:S(2)}, u32[]{:S(2)}) async-start(bf16[8,4,32,2048]{3,2,0,1:T(8,128)(2,1)} %bitcast.56), calls=%async_computation.3 | async-start | bytes 8388608 | tf_op jit(solution)/shard_map/all_to_all | solution.py:71
  326.0 0.1 and.24
  326.1 0.0 copy-done.2
  326.1 0.1 copy.31
  326.2 47.7 %all-to-all-done.3 = bf16[8,4,32,2048]{3,2,0,1:T(8,128)(2,1)} async-done(((bf16[8,4,32,2048]{3,2,0,1:T(8,128)(2,1)}), bf16[8,4,32,2048]{3,2,0,1:T(8,128)(2,1)}, u32[]{:S(2)}, u32[]{:S(2)}) %all-to-all-start.3) | async-done | bytes 4194336 | tf_op jit(solution)/shard_map/all_to_all | solution.py:71
  373.9 4.7 %copy.37 = bf16[8,4,32,2048]{3,2,1,0:T(8,128)(2,1)} copy(bf16[8,4,32,2048]{3,2,0,1:T(8,128)(2,1)} %all-to-all-done.3) | data formatting | bytes 8388608 | tf_op jit(solution)/shard_map/all_to_all | solution.py:71
  378.7 0.0 copy-start.1
  378.7 11.7 %gather_fusion = bf16[1024,2048]{1,0:T(8,128)(2,1)} fusion(bf16[1024,2048]{1,0:T(8,128)(2,1)} %bitcast.54, s32[1024]{0:T(1024)S(1)} %broadcast_clamp_fusion), kind=kCustom, calls=%fused_computation | custom fusion | bytes 8392704 | tf_op jit(solution)/shard_map/gather | solution.py:85
  390.4 7.3 %fusion = bf16[128,2048]{1,0:T(8,128)(2,1)} fusion(bf16[1024,2048]{1,0:T(8,128)(2,1)} %gather_fusion, f32[128,8]{1,0:T(8,128)S(1)} %broadcast_select_fusion), kind=kLoop, calls=%fused_computation.4 | loop fusion | flops 6029312 | bytes 4722688 | tf_op jit(solution)/shard_map/reduce_sum | solution.py:87
  397.7 0.0 copy-done.1
  (9 shorter events, 0.1 us)
Async XLA Ops:
  0.0 201.6 %copy-start = (bf16[1,384,2048]{2,1,0:T(8,128)(2,1)S(1)}, bf16[1,384,2048]{2,1,0:T(8,128)(2,1)}, u32[]{:S(2)}) copy-start(bf16[1,384,2048]{2,1,0:T(8,128)(2,1)} %param.13) | copy-start | bytes 4718596
  134.2 58.0 %copy-start.3 = (bf16[1,2048,384]{2,1,0:T(8,128)(2,1)S(1)}, bf16[1,2048,384]{2,1,0:T(8,128)(2,1)}, u32[]{:S(2)}) copy-start(bf16[1,2048,384]{2,1,0:T(8,128)(2,1)} %param.11) | copy-start | bytes 4718596
  185.1 11.8 %copy-start.4 = (bf16[1,2048,384]{2,1,0:T(8,128)(2,1)S(1)}, bf16[1,2048,384]{2,1,0:T(8,128)(2,1)}, u32[]{:S(2)}) copy-start(bf16[1,2048,384]{2,1,0:T(8,128)(2,1)} %param.12) | copy-start | bytes 4718596
  185.1 7.2 %collective-permute-start = (bf16[1024,2048]{1,0:T(8,128)(2,1)S(1)}, bf16[1024,2048]{1,0:T(8,128)(2,1)S(1)}, u32[]{:S(2)}, u32[]{:S(2)}) collective-permute-start(bf16[1024,2048]{1,0:T(8,128)(2,1)S(1)} %bitcast.61), channel_id=1, source_target_pairs={{0,1},{1,0},{2,3},{3,2},{4,5},{5,4},{6,7},{7,6},{8,9},{9,8},{10,11... | collective-permute-start | bytes 12582920 | tf_op jit(solution)/shard_map/ppermute | solution.py:14
  206.9 7.2 %collective-permute-start.1 = (bf16[1024,2048]{1,0:T(8,128)(2,1)S(1)}, bf16[1024,2048]{1,0:T(8,128)(2,1)S(1)}, u32[]{:S(2)}, u32[]{:S(2)}) collective-permute-start(bf16[1024,2048]{1,0:T(8,128)(2,1)S(1)} %slice.21), channel_id=1, source_target_pairs={{0,1},{1,0},{2,3},{3,2},{4,5},{5,4},{6,7},{7,6},{8,9},{9,8},{10,11... | collective-permute-start | bytes 12582920 | tf_op jit(solution)/shard_map/ppermute | solution.py:14
  320.7 5.4 %copy-start.2 = (f32[128,8]{0,1:T(8,128)S(1)}, f32[128,8]{0,1:T(8,128)}, u32[]{:S(2)}) copy-start(f32[128,8]{0,1:T(8,128)} %param.9) | copy-start | bytes 12292
  320.7 53.2 %all-to-all-start.3 = ((bf16[8,4,32,2048]{3,2,0,1:T(8,128)(2,1)}), bf16[8,4,32,2048]{3,2,0,1:T(8,128)(2,1)}, u32[]{:S(2)}, u32[]{:S(2)}) async-start(bf16[8,4,32,2048]{3,2,0,1:T(8,128)(2,1)} %bitcast.56), calls=%async_computation.3 | async-start | bytes 8388608 | tf_op jit(solution)/shard_map/all_to_all | solution.py:71
  378.7 19.0 %copy-start.1 = (bf16[1,384,2048]{2,1,0:T(8,128)(2,1)S(1)}, bf16[1,384,2048]{2,1,0:T(8,128)(2,1)}, u32[]{:S(2)}) copy-start(bf16[1,384,2048]{2,1,0:T(8,128)(2,1)} %param.13) | copy-start | bytes 4718596
where the time goes:
time: 398 us
  blocking collectives  263 us (66%)
  waiting for transfers between devices  61.9 us (16%)
  local copies, waits for them, and re-layouts  36 us (9%)
  other arithmetic  16.6 us (4%)
  matrix products  14.3 us (4%)
  starting transfers between devices  5.46 us (1%)
    all_to_all x1, blocking collectives, on_device(): lax.all_to_all(merged.reshape(1, col_size, -1, feature_width), 'dp', spli...  96.8 us
    all_to_all x1, blocking collectives, on_device(): lax.all_to_all(sendbuf, 'dp', split_axis=0, concat_axis=2, tiled=True)  93.3 us
    all_to_all x1, blocking collectives, on_device(): lax.all_to_all(lax.all_to_all(sendbuf, 'dp', split_axis=0, concat_axis=2,...  50.9 us
    all_to_all x1, waiting for transfers between devices, on_device(): lax.all_to_all(lax.all_to_all(merged.reshape(1, col_size, -1, feature_wid...  47.7 us
    all_gather x1, blocking collectives, on_device(): count_table = lax.all_gather(kept_count[None, :], 'dp', axis=0, tiled=True)  22.3 us
    ppermute x2, waiting for transfers between devices, partner_2(): return lax.ppermute(block, axis, route)  14.2 us
    gather x1, local copies, waits for them, and re-layouts, on_device(): results[jnp.minimum(position, slots_total - 1)].astype(jnp.float32)  11.7 us
    scatter x1, local copies, waits for them, and re-layouts, on_device(): jnp.zeros((slots_total, feature_width), jnp.bfloat16).at[position]  9.45 us
  transfers between devices with their start and end apart: 3, of which 3 were waited for; matrix products, arithmetic and copies ran while one was open for 0% of the time, Pallas kernels for 0%

commit v1 on v0

v1 whole, which is shorter than its diff:
```python
import jax
import jax.numpy as jnp
from jax import lax
from jax.sharding import PartitionSpec as P

BF = jnp.bfloat16
F32 = jnp.float32
CHUNKS = 2


def swap_cores(block, col_size):
    return lax.ppermute(block, "expert", [(c, c ^ 1) for c in range(col_size)])


def turn(block, col_size, by):
    route = [(c, (c + 2 * by) % col_size) for c in range(col_size)]
    return lax.ppermute(block, "expert", route)


def slot_matrices(ids, probs, limits, col_cap, per_row):
    dp_size, tok_rows, _ = ids.shape
    count_y = per_row
    first = lax.axis_index("dp") * per_row
    here = lax.axis_index("expert") // 2
    wanted = first + lax.rem(here + jnp.arange(count_y, dtype=jnp.int32), count_y)
    match = ids[None] == wanted.astype(F32)[:, None, None, None]
    chosen = jnp.sum(match.astype(F32), axis=3)
    weight = jnp.sum(jnp.where(match, probs[None], 0.0), axis=3)
    lower = (jnp.arange(tok_rows)[:, None] < jnp.arange(tok_rows)[None, :]).astype(BF)
    rank = jnp.dot(
        chosen.reshape(-1, tok_rows).astype(BF), lower, preferred_element_type=F32
    ).reshape(chosen.shape)
    pick = (jnp.arange(limits.shape[1], dtype=jnp.int32)[None, :] == wanted[:, None]).astype(F32)
    limit = jnp.sum(pick[:, None, :] * limits[None], axis=2)
    kept = jnp.minimum(jnp.sum(chosen, axis=2), limit)
    earlier = (jnp.arange(dp_size)[:, None] < jnp.arange(dp_size)[None, :]).astype(F32)
    offset = jnp.sum(kept[:, :, None] * earlier[None], axis=1)
    slot = offset[:, :, None] + rank
    keep = (chosen > 0) & (rank < limit[:, :, None]) & (slot < col_cap)
    slot = jnp.where(keep, slot, float(col_cap)).astype(jnp.int32).reshape(count_y, 1, -1)
    weight = weight.reshape(count_y, 1, -1)
    spot = jnp.arange(col_cap, dtype=jnp.int32)[None, :, None] == slot
    return spot.astype(BF), jnp.where(spot, weight, 0.0).astype(BF)


def on_device(tokens, expert_ids, route_probs, shard_limit, gate_proj, up_proj, down_proj):
    tok_rows, width = tokens.shape
    top = expert_ids.shape[1]
    experts = shard_limit.shape[1]
    dp_size = lax.axis_size("dp")
    col_size = lax.axis_size("expert")
    per_row = col_size // 2
    capacity = tok_rows * top // experts
    col_cap = dp_size * capacity // 2
    part = width // CHUNKS

    used = 2 * top + experts
    meta = jnp.concatenate(
        [
            expert_ids.astype(BF),
            route_probs.astype(BF),
            jnp.broadcast_to(shard_limit.astype(BF), (tok_rows, experts)),
            jnp.zeros((tok_rows, -used % 128), BF),
        ],
        axis=1,
    )
    first = lax.all_gather(
        jnp.concatenate([tokens[:, :part], meta], axis=1), "dp", axis=0, tiled=True
    )
    columns = [first[:, :part]]
    for n in range(1, CHUNKS):
        columns.append(
            lax.all_gather(tokens[:, n * part : (n + 1) * part], "dp", axis=0, tiled=True)
        )
    info = first[:, part:].reshape(dp_size, tok_rows, -1).astype(F32)
    spots, weights = slot_matrices(
        info[:, :, :top],
        info[:, :, top : 2 * top],
        info[:, 0, 2 * top : used],
        col_cap,
        per_row,
    )

    gate_half, up_half, down_half = gate_proj[0], up_proj[0], down_proj[0]
    stacks = []
    for n in range(CHUNKS):
        slots = jnp.einsum("rst,td->rsd", spots, columns[n], preferred_element_type=F32).astype(BF)
        held = [slots[0]] + [turn(slots[r], col_size, r) for r in range(1, per_row)]
        held = jnp.concatenate(held, axis=0)
        stacks.append(jnp.concatenate([held, swap_cores(held, col_size)], axis=0))
    rows = jnp.concatenate(stacks, axis=1)
    gate_val = jnp.dot(rows, gate_half, preferred_element_type=F32)
    up_val = jnp.dot(rows, up_half, preferred_element_type=F32)
    hidden = (jax.nn.silu(gate_val) * up_val).astype(BF)

    own = per_row * col_cap
    outs = []
    for n in range(CHUNKS):
        partial = jnp.dot(
            hidden, down_half[:, n * part : (n + 1) * part], preferred_element_type=F32
        ).astype(BF)
        back = swap_cores(partial[own:], col_size)
        merged = (partial[:own].astype(F32) + back.astype(F32)).astype(BF)
        merged = merged.reshape(per_row, col_cap, part)
        home = [merged[0]] + [turn(merged[r], col_size, -r) for r in range(1, per_row)]
        home = jnp.stack(home, axis=0)
        mixed = jnp.einsum("rst,rsd->td", weights, home, preferred_element_type=F32).astype(BF)
        outs.append(lax.psum_scatter(mixed, "dp", scatter_dimension=0, tiled=True))
    return jnp.concatenate(outs, axis=1)


def solution(mesh):
    rows = P(("dp", "expert"), None)
    blocks = P(("dp", "expert"), None, None)
    return jax.shard_map(
        on_device,
        mesh=mesh,
        in_specs=(rows, rows, rows, rows, blocks, blocks, blocks),
        out_specs=rows,
        check_vma=False,
    )
```

time: 398 us -> 308 us (0.77)
  blocking collectives: 263 us -> 0 us
  waiting for transfers between devices: 61.9 us -> 256 us
  local copies, waits for them, and re-layouts: 36 us -> 6.22 us
  between operations: 0.17 us -> 13.4 us
  other arithmetic: 16.6 us -> 5.45 us
  matrix products: 14.3 us -> 19.5 us
    all_to_all x3 -> x0, blocking collectives: 241 us -> none  [the longest x1 96.8 us: on_device(): lax.all_to_all(merged.reshape(1, col_size, -1, feature_width), 'dp', spli...]
    reduce_scatter x0 -> x2, waiting for transfers between devices: none -> 116 us  [on_device(): outs.append(lax.psum_scatter(mixed, 'dp', scatter_dimension=0, tiled=True))]
    all_gather x0 -> x2, waiting for transfers between devices: none -> 96.9 us  [the longest x1 53.8 us: on_device(): lax.all_gather(jnp.concatenate([tokens[:, :part], meta], axis=1), 'dp', a...]
    all_to_all x1 -> x0, waiting for transfers between devices: 47.7 us -> none  [on_device(): lax.all_to_all(lax.all_to_all(merged.reshape(1, col_size, -1, feature_wid...]
    ppermute x2 -> x8, waiting for transfers between devices: 14.2 us -> 42.9 us  [the longest x4 35.1 us: turn(): return lax.ppermute(block, 'expert', route)]
    all_gather x1 -> x0, blocking collectives: 22.3 us -> none  [on_device(): count_table = lax.all_gather(kept_count[None, :], 'dp', axis=0, tiled=True)]
    gather x1 -> x0, local copies, waits for them, and re-layouts: 11.7 us -> none  [on_device(): results[jnp.minimum(position, slots_total - 1)].astype(jnp.float32)]
    all_to_all x3 -> x0, local copies, waits for them, and re-layouts: 9.58 us -> none  [the longest x1 4.74 us: on_device(): lax.all_to_all(lax.all_to_all(merged.reshape(1, col_size, -1, feature_wid...]
  transfers between devices with their start and end apart: 3 -> 12, of which waited for: 3 -> 10; matrix products, arithmetic and copies ran while one was open for 0% -> 5% of each run, Pallas kernels for 0% -> 0%
where the time goes in v1:
time: 308 us; the launch traced here: 307 us
  waiting for transfers between devices  256 us (83%)
  matrix products  19.5 us (6%)
  between operations  13.4 us (4%)
  starting transfers between devices  6.68 us (2%)
  local copies, waits for them, and re-layouts  6.22 us (2%)
  other arithmetic  5.45 us (2%)
    reduce_scatter x2, waiting for transfers between devices, on_device(): outs.append(lax.psum_scatter(mixed, 'dp', scatter_dimension=0, tiled=True))  116 us
    all_gather x1, waiting for transfers between devices, on_device(): lax.all_gather(jnp.concatenate([tokens[:, :part], meta], axis=1), 'dp', a...  53.8 us
    all_gather x1, waiting for transfers between devices, on_device(): lax.all_gather(tokens[:, n * part:(n + 1) * part], 'dp', axis=0, tiled=True)  43.1 us
    ppermute x4, waiting for transfers between devices, turn(): return lax.ppermute(block, 'expert', route)  35.1 us
    ppermute x4, waiting for transfers between devices, swap_cores(): return lax.ppermute(block, 'expert', [(c, c ^ 1) for c in range(col_size)])  7.81 us
  transfers between devices with their start and end apart: 12, of which 10 were waited for; matrix products, arithmetic and copies ran while one was open for 5% of the time, Pallas kernels for 0%

profile of v1, /device:TPU:0, one launch (start us, length us, event | category | flops | bytes accessed | tf_op | source)
XLA Modules:
  0.0 307.4 jit_solution(12723814263804080153)
XLA Ops:
  6.5 0.8 convert_bitcast_fusion.1
  7.3 0.7 convert_element_type.90
  8.0 0.7 convert_element_type.91
  8.7 0.1 copy.14
  8.8 0.1 copy.13
  8.9 1.8 fusion.45
  10.7 0.8 concatenate.23
  11.6 0.0 all-gather.3.cloned.1.call-update
  11.6 0.0 all-gather.5.cloned.1.call-start
  11.6 0.7 all-gather.5.cloned.1.call-update
  12.3 0.0 reduce-scatter.5.cloned.1.call-start
  12.4 0.1 compare_convert_fusion
  12.5 53.8 %all-gather.3.cloned.1.call-done = bf16[1024,1152]{1,0:T(8,128)(2,1)} async-done(((bf16[128,1152]{1,0:T(8,128)(2,1)}), bf16[1024,1152]{1,0:T(8,128)(2,1)}) %all-gather.3.cloned.1.call-update) | async-done | bytes 2359312 | tf_op jit(solution)/shard_map/all_gather | solution.py:67
  66.3 1.0 slice.94
  67.3 0.1 slice.96
  67.3 0.1 fusion.46
  67.5 0.2 copy.15
  67.6 0.2 copy.17
  67.8 0.1 multiply_reduce_fusion.1
  67.9 0.2 fusion.27
  68.1 0.1 multiply_reduce_fusion
  68.2 0.1 convert_bitcast_fusion
  68.3 0.1 copy.28
  68.4 3.0 fusion.10
  71.4 0.1 slice_bitcast_fusion.9
  71.4 1.5 collective-permute-start
  73.0 43.1 %all-gather.5.cloned.1.call-done = bf16[1024,1024]{1,0:T(8,128)(2,1)} async-done(((bf16[128,1024]{1,0:T(8,128)(2,1)}), bf16[1024,1024]{1,0:T(8,128)(2,1)}) %all-gather.5.cloned.1.call-update) | async-done | bytes 2097168 | tf_op jit(solution)/shard_map/all_gather | solution.py:73
  116.1 3.0 fusion.7
  119.0 0.1 slice_bitcast_fusion.7
  119.1 1.5 collective-permute-start.2
  120.6 0.1 pad_maximum_fusion
  120.7 0.1 collective-permute-start.1
  120.8 10.1 %collective-permute-done.2 = bf16[256,1024]{1,0:T(8,128)(2,1)S(1)} collective-permute-done((bf16[256,1024]{1,0:T(8,128)(2,1)S(1)}, bf16[256,1024]{1,0:T(8,128)(2,1)S(1)}, u32[]{:S(2)}, u32[]{:S(2)}) %collective-permute-start.2) | collective-permute-done | bytes 524320 | tf_op jit(solution)/shard_map/ppermute | solution.py:17
  130.9 0.1 pad_maximum_fusion.1
  131.0 0.0 copy-start.1
  131.0 0.1 collective-permute-start.3
  131.1 2.6 collective-permute-done.3
  133.7 2.3 fusion.5
  136.1 2.4 multiply_convert_fusion
  138.5 1.2 convolution_convert_fusion
  139.8 0.1 slice.110
  139.9 0.2 collective-permute-start.6
  140.1 2.5 collective-permute-done.6
  142.6 0.4 add_convert_fusion
  143.0 0.1 slice_bitcast_fusion.4
  143.1 1.5 collective-permute-start.7
  144.7 12.5 %collective-permute-done.7 = bf16[256,1024]{1,0:T(8,128)(2,1)S(1)} collective-permute-done((bf16[256,1024]{1,0:T(8,128)(2,1)S(1)}, bf16[256,1024]{1,0:T(8,128)(2,1)S(1)}, u32[]{:S(2)}, u32[]{:S(2)}) %collective-permute-start.7) | collective-permute-done | bytes 524320 | tf_op jit(solution)/shard_map/ppermute | solution.py:17
  157.1 2.5 bitcast_convert_fusion
  159.7 0.0 reduce-scatter.5.cloned.1.call-update
  159.7 0.0 reduce-scatter.3.cloned.1.call-start
  159.7 1.3 copy-done.3
  161.1 2.4 convolution_convert_fusion.1
  163.5 0.1 slice.105
  163.5 0.1 collective-permute-start.4
  163.6 2.6 collective-permute-done.4
  166.3 0.4 add_convert_fusion.1
  166.7 0.1 slice_bitcast_fusion.5
  166.8 1.5 collective-permute-start.5
  168.3 12.5 %collective-permute-done.5 = bf16[256,1024]{1,0:T(8,128)(2,1)S(1)} collective-permute-done((bf16[256,1024]{1,0:T(8,128)(2,1)S(1)}, bf16[256,1024]{1,0:T(8,128)(2,1)S(1)}, u32[]{:S(2)}, u32[]{:S(2)}) %collective-permute-start.5) | collective-permute-done | bytes 524320 | tf_op jit(solution)/shard_map/ppermute | solution.py:17
  180.8 2.5 bitcast_convert_fusion.1
  183.3 0.0 reduce-scatter.3.cloned.1.call-update
  183.3 44.8 %reduce-scatter.5.cloned.1.call-done = bf16[128,1024]{1,0:T(8,128)(2,1)} async-done(((bf16[1024,1024]{1,0:T(8,128)(2,1)}), bf16[128,1024]{1,0:T(8,128)(2,1)}) %reduce-scatter.5.cloned.1.call-update) | async-done | bytes 262160 | tf_op jit(solution)/shard_map/reduce_scatter | solution.py:108
  228.1 70.9 %reduce-scatter.3.cloned.1.call-done = bf16[128,1024]{1,0:T(8,128)(2,1)} async-done(((bf16[1024,1024]{1,0:T(8,128)(2,1)}), bf16[128,1024]{1,0:T(8,128)(2,1)}) %reduce-scatter.3.cloned.1.call-update) | async-done | bytes 262160 | tf_op jit(solution)/shard_map/reduce_scatter | solution.py:108
  299.0 1.9 pad_maximum_fusion.2
  (17 shorter events, 0.1 us)
Async XLA Ops:
  6.5 127.2 %copy-start = (bf16[1,2048,384]{2,1,0:T(8,128)(2,1)S(1)}, bf16[1,2048,384]{2,1,0:T(8,128)(2,1)}, u32[]{:S(2)}) copy-start(bf16[1,2048,384]{2,1,0:T(8,128)(2,1)} %param.11) | copy-start | bytes 4718596
  6.5 59.7 %all-gather.3.cloned.1.call-start = ((), (), s32[]{:S(2)}) async-start(), calls=%async_computation.2 | async-start | bytes 2654208 | tf_op jit(solution)/shard_map/all_gather | solution.py:67
  11.6 104.5 %all-gather.5.cloned.1.call-start = ((), (), s32[]{:S(2)}) async-start(), calls=%async_computation.3 | async-start | bytes 2359296 | tf_op jit(solution)/shard_map/all_gather | solution.py:73
  12.3 215.8 %reduce-scatter.5.cloned.1.call-start = ((), (), s32[]{:S(2)}) async-start(), calls=%async_computation.5 | async-start | bytes 2359296 | tf_op jit(solution)/shard_map/reduce_scatter | solution.py:108
  71.4 49.2 %collective-permute-start = (bf16[256,1024]{1,0:T(8,128)(2,1)S(1)}, bf16[256,1024]{1,0:T(8,128)(2,1)S(1)}, u32[]{:S(2)}, u32[]{:S(2)}) collective-permute-start(bf16[256,1024]{1,0:T(8,128)(2,1)S(1)} %get-tuple-element.15), channel_id=1, source_target_pairs={{0,2},{1,3},{2,0},{3,1},{4,6},{5,7},{6,4},{7,5},{8,10},{9,11},{10,... | collective-permute-start | bytes 1572872 | tf_op jit(solution)/shard_map/ppermute | solution.py:17
  119.1 11.8 %collective-permute-start.2 = (bf16[256,1024]{1,0:T(8,128)(2,1)S(1)}, bf16[256,1024]{1,0:T(8,128)(2,1)S(1)}, u32[]{:S(2)}, u32[]{:S(2)}) collective-permute-start(bf16[256,1024]{1,0:T(8,128)(2,1)S(1)} %get-tuple-element.17), channel_id=1, source_target_pairs={{0,2},{1,3},{2,0},{3,1},{4,6},{5,7},{6,4},{7,5},{8,10},{9,11},{10,... | collective-permute-start | bytes 1572872 | tf_op jit(solution)/shard_map/ppermute | solution.py:17
  120.7 10.4 %collective-permute-start.1 = (bf16[512,1024]{1,0:T(8,128)(2,1)S(1)}, bf16[512,1024]{1,0:T(8,128)(2,1)S(1)}, u32[]{:S(2)}, u32[]{:S(2)}) collective-permute-start(bf16[512,1024]{1,0:T(8,128)(2,1)S(1)} %pad_maximum_fusion), channel_id=1, source_target_pairs={{0,1},{1,0},{2,3},{3,2},{4,5},{5,4},{6,7},{7,6},{8,9},{9,8},{10,11... | collective-permute-start | bytes 3145736 | tf_op jit(solution)/shard_map/ppermute | solution.py:12
  131.0 5.1 %copy-start.1 = (bf16[1,2048,384]{2,1,0:T(8,128)(2,1)S(1)}, bf16[1,2048,384]{2,1,0:T(8,128)(2,1)}, u32[]{:S(2)}) copy-start(bf16[1,2048,384]{2,1,0:T(8,128)(2,1)} %param.12) | copy-start | bytes 4718596
  131.0 2.7 collective-permute-start.3
  136.1 2.5 copy-start.2
  138.5 1.4 copy-start.4
  139.9 2.7 collective-permute-start.6
  143.1 14.0 %collective-permute-start.7 = (bf16[256,1024]{1,0:T(8,128)(2,1)S(1)}, bf16[256,1024]{1,0:T(8,128)(2,1)S(1)}, u32[]{:S(2)}, u32[]{:S(2)}) collective-permute-start(bf16[256,1024]{1,0:T(8,128)(2,1)S(1)} %get-tuple-element.13), channel_id=1, source_target_pairs={{0,2},{1,3},{2,0},{3,1},{4,6},{5,7},{6,4},{7,5},{8,10},{9,11},{10,... | collective-permute-start | bytes 1572872 | tf_op jit(solution)/shard_map/ppermute | solution.py:17
  159.7 1.4 copy-start.3
  159.7 139.3 %reduce-scatter.3.cloned.1.call-start = ((), (), s32[]{:S(2)}) async-start(), calls=%async_computation.4 | async-start | bytes 2359296 | tf_op jit(solution)/shard_map/reduce_scatter | solution.py:108
  163.5 2.7 collective-permute-start.4
  166.8 14.0 %collective-permute-start.5 = (bf16[256,1024]{1,0:T(8,128)(2,1)S(1)}, bf16[256,1024]{1,0:T(8,128)(2,1)S(1)}, u32[]{:S(2)}, u32[]{:S(2)}) collective-permute-start(bf16[256,1024]{1,0:T(8,128)(2,1)S(1)} %get-tuple-element.11), channel_id=1, source_target_pairs={{0,2},{1,3},{2,0},{3,1},{4,6},{5,7},{6,4},{7,5},{8,10},{9,11},{10,... | collective-permute-start | bytes 1572872 | tf_op jit(solution)/shard_map/ppermute | solution.py:17
Sparse Core Ops, SparseCore 0:
  11.7 54.5 all-gather.2
  68.4 47.6 all-gather.4
  159.8 68.2 reduce-scatter.4
  231.5 67.4 reduce-scatter.2

commit v2 on v1

--- a/solution.py
+++ b/solution.py
@@ -1,11 +1,260 @@
+import functools
+
 import jax
 import jax.numpy as jnp
 from jax import lax
+from jax.experimental import pallas as pl
+from jax.experimental.pallas import tpu as pltpu
 from jax.sharding import PartitionSpec as P
 
 BF = jnp.bfloat16
 F32 = jnp.float32
 CHUNKS = 2
+
+
+class Wires:
+    def __init__(self, ssem, rsem):
+        self.ssem, self.rsem = ssem, rsem
+        self.count = 0
+        self.sent = []
+
+    def lane(self):
+        self.count += 1
+        return self.count - 1
+
+    def copy(self, src, dst, lane, to):
+        return pltpu.make_async_remote_copy(
+            src_ref=src,
+            dst_ref=dst,
+            send_sem=self.ssem.at[lane],
+            recv_sem=self.rsem.at[lane],
+            device_id={"dp": to},
+            device_id_type=pl.DeviceIdType.MESH,
+        )
+
+    def send(self, src, dst, lane, to):
+        moved = self.copy(src, dst, lane, to)
+        moved.start()
+        self.sent.append(moved)
+
+    def arrive(self, dst, lane, to):
+        self.copy(dst, dst, lane, to).wait_recv()
+
+    def finish(self):
+        for moved in self.sent:
+            moved.wait_send()
+
+
+def places(ring):
+    me = lax.axis_index("dp")
+    z, x = lax.div(me, 2), lax.rem(me, 2)
+    ahead = lax.rem(z + 1, ring) * 2 + x
+    behind = lax.rem(z + ring - 1, ring) * 2 + x
+    return z, x, ahead, behind, z * 2 + 1 - x
+
+
+def greet(peers):
+    barrier = pltpu.get_barrier_semaphore()
+    for peer in peers:
+        pl.semaphore_signal(
+            barrier, inc=1, device_id={"dp": peer}, device_id_type=pl.DeviceIdType.MESH
+        )
+    pl.semaphore_wait(barrier, len(peers))
+
+
+def gather_kernel(ring, src, out, ssem, rsem, own_sem):
+    z, x, ahead, behind, other = places(ring)
+    greet((ahead, behind, other))
+    rows = src.shape[0]
+    piece = rows // 4
+    wires = Wires(ssem, rsem)
+    to = [ahead, behind]
+
+    def at(zz, xx, k):
+        start = pl.multiple_of((zz * 2 + xx) * rows + k * piece, piece)
+        return out.at[pl.ds(start, piece)]
+
+    def back(k, s):
+        return lax.rem(z + (ring - s if k % 2 == 0 else s), ring)
+
+    own = [src.at[pl.ds(k * piece, piece)] for k in range(4)]
+    ring_lane = {}
+    for k in range(4):
+        for s in range(ring - 1):
+            ring_lane[k, 0, s] = wires.lane()
+            if k >= 2:
+                ring_lane[k, 1, s] = wires.lane()
+    cross_lane = {}
+    for k in range(4):
+        for s in range(ring if k < 2 else 1):
+            cross_lane[k, s] = wires.lane()
+
+    for k in (2, 3):
+        wires.send(own[k], at(z, x, k), cross_lane[k, 0], other)
+    for k in range(4):
+        wires.send(own[k], at(z, x, k), ring_lane[k, 0, 0], to[k % 2])
+    for k in (0, 1):
+        wires.send(own[k], at(z, x, k), cross_lane[k, 0], other)
+    local = pltpu.make_async_copy(
+        src, out.at[pl.ds(pl.multiple_of((z * 2 + x) * rows, rows), rows)], own_sem
+    )
+    local.start()
+    for k in (2, 3):
+        block = at(z, 1 - x, k)
+        wires.arrive(block, cross_lane[k, 0], other)
+        wires.send(block, block, ring_lane[k, 1, 0], to[k % 2])
+    for s in range(ring - 1):
+        for k in (0, 1):
+            block = at(back(k, s + 1), x, k)
+            wires.arrive(block, ring_lane[k, 0, s], other)
+            if s < ring - 2:
+                wires.send(block, block, ring_lane[k, 0, s + 1], to[k % 2])
+            wires.send(block, block, cross_lane[k, s + 1], other)
+        for j in range(2):
+            for k in (2, 3):
+                block = at(back(k, s + 1), x if j == 0 else 1 - x, k)
+                wires.arrive(block, ring_lane[k, j, s], other)
+                if s < ring - 2:
+                    wires.send(block, block, ring_lane[k, j, s + 1], to[k % 2])
+    for s in range(ring):
+        for k in (0, 1):
+            wires.arrive(at(back(k, s), 1 - x, k), cross_lane[k, s], other)
+    local.wait()
+    wires.finish()
+
+
+def scatter_kernel(ring, part, out, cross_a, ring_a, ring_b, cross_b, ssem, rsem):
+    z, x, ahead, behind, other = places(ring)
+    greet((ahead, behind, other))
+    rows = out.shape[0]
+    piece = rows // 4
+    wires = Wires(ssem, rsem)
+    to = [ahead, behind]
+
+    def at(zz, xx, k):
+        start = pl.multiple_of((zz * 2 + xx) * rows + k * piece, piece)
+        return part.at[pl.ds(start, piece)]
+
+    def goal(k, s):
+        return lax.rem(z + (ring - 1 - s if k % 2 == 0 else 1 + s), ring)
+
+    def total(*refs):
+        value = refs[0][...].astype(F32)
+        for ref in refs[1:]:
+            value = value + ref[...].astype(F32)
+        return value.astype(BF)
+
+    lanes = {}
+    for k in range(4):
+        for s in range(ring - 1):
+            lanes[k, 0, s] = wires.lane()
+            if k >= 2:
+                lanes[k, 1, s] = wires.lane()
+        for s in range(ring if k < 2 else 1):
+            lanes["c", k, s] = wires.lane()
+
+    for j in range(2):
+        for k in (2, 3):
+            wires.send(
+                at(goal(k, 0), x if j == 0 else 1 - x, k),
+                ring_b.at[k - 2, j, 0],
+                lanes[k, j, 0],
+                to[k % 2],
+            )
+    for s in range(ring):
+        for k in (0, 1):
+            wires.send(
+                at(goal(k, s), 1 - x, k), cross_a.at[k, s], lanes["c", k, s], other
+            )
+    for s in range(ring - 1):
+        for k in (0, 1):
+            mine = cross_a.at[k, s]
+            wires.arrive(mine, lanes["c", k, s], other)
+            terms = [mine, at(goal(k, s), x, k)]
+            if s > 0:
+                came = ring_a.at[k, s - 1]
+                wires.arrive(came, lanes[k, 0, s - 1], other)
+                terms.append(came)
+            mine[...] = total(*terms)
+            wires.send(mine, ring_a.at[k, s], lanes[k, 0, s], to[k % 2])
+        if s > 0:
+            for j in (1, 0):
+                for k in (2, 3):
+                    came = ring_b.at[k - 2, j, s - 1]
+                    wires.arrive(came, lanes[k, j, s - 1], other)
+                    came[...] = total(came, at(goal(k, s), x if j == 0 else 1 - x, k))
+                    wires.send(came, ring_b.at[k - 2, j, s], lanes[k, j, s], to[k % 2])
+    for k in (2, 3):
+        came = ring_b.at[k - 2, 1, ring - 2]
+        wires.arrive(came, lanes[k, 1, ring - 2], other)
+        came[...] = total(came, at(z, 1 - x, k))
+        wires.send(came, cross_b.at[k - 2], lanes["c", k, 0], other)
+    for k in (0, 1):
+        wires.arrive(cross_a.at[k, ring - 1], lanes["c", k, ring - 1], other)
+        wires.arrive(ring_a.at[k, ring - 2], lanes[k, 0, ring - 2], other)
+        out[pl.ds(k * piece, piece)] = total(
+            at(z, x, k), cross_a.at[k, ring - 1], ring_a.at[k, ring - 2]
+        )
+    for k in (2, 3):
+        came = ring_b.at[k - 2, 0, ring - 2]
+        wires.arrive(came, lanes[k, 0, ring - 2], other)
+        wires.arrive(cross_b.at[k - 2], lanes["c", k, 0], other)
+        out[pl.ds(k * piece, piece)] = total(at(z, x, k), came, cross_b.at[k - 2])
+    wires.finish()
+
+
+def kernel_params(number):
+    return pltpu.CompilerParams(
+        collective_id=number, has_side_effects=True, vmem_limit_bytes=48 << 20
+    )
+
+
+VM = pl.BlockSpec(memory_space=pltpu.VMEM)
+
+
+def gather_dp(block, number):
+    dp_size = lax.axis_size("dp")
+    ring = dp_size // 2
+    count = 8 * ring - 4
+    return pl.pallas_call(
+        functools.partial(gather_kernel, ring),
+        name="gather%d" % number,
+        out_shape=jax.ShapeDtypeStruct((dp_size * block.shape[0], block.shape[1]), block.dtype),
+        in_specs=[VM],
+        out_specs=VM,
+        scratch_shapes=[
+            pltpu.SemaphoreType.DMA((count,)),
+            pltpu.SemaphoreType.DMA((count,)),
+            pltpu.SemaphoreType.DMA,
+        ],
+        compiler_params=kernel_params(number),
+        cost_estimate=pl.CostEstimate(flops=0, transcendentals=0, bytes_accessed=60 << 20),
+    )(block)
+
+
+def scatter_dp(parts, number):
+    dp_size = lax.axis_size("dp")
+    ring = dp_size // 2
+    rows, wide = parts.shape[0] // dp_size, parts.shape[1]
+    piece = rows // 4
+    count = 8 * ring - 4
+    return pl.pallas_call(
+        functools.partial(scatter_kernel, ring),
+        name="scatter%d" % number,
+        out_shape=jax.ShapeDtypeStruct((rows, wide), parts.dtype),
+        in_specs=[VM],
+        out_specs=VM,
+        scratch_shapes=[
+            pltpu.VMEM((2, ring, piece, wide), BF),
+            pltpu.VMEM((2, ring - 1, piece, wide), BF),
+            pltpu.VMEM((2, 2, ring - 1, piece, wide), BF),
+            pltpu.VMEM((2, piece, wide), BF),
+            pltpu.SemaphoreType.DMA((count,)),
+            pltpu.SemaphoreType.DMA((count,)),
+        ],
+        compiler_params=kernel_params(number),
+        cost_estimate=pl.CostEstimate(flops=0, transcendentals=0, bytes_accessed=60 << 20),
+    )(parts)
 
 
 def swap_cores(block, col_size):
@@ -64,14 +313,10 @@
         ],
         axis=1,
     )
-    first = lax.all_gather(
-        jnp.concatenate([tokens[:, :part], meta], axis=1), "dp", axis=0, tiled=True
-    )
+    first = gather_dp(jnp.concatenate([tokens[:, :part], meta], axis=1), 0)
     columns = [first[:, :part]]
     for n in range(1, CHUNKS):
-        columns.append(
-            lax.all_gather(tokens[:, n * part : (n + 1) * part], "dp", axis=0, tiled=True)
-        )
+        columns.append(gather_dp(tokens[:, n * part : (n + 1) * part], 2 * n))
     info = first[:, part:].reshape(dp_size, tok_rows, -1).astype(F32)
     spots, weights = slot_matrices(
         info[:, :, :top],
@@ -105,7 +350,7 @@
         home = [merged[0]] + [turn(merged[r], col_size, -r) for r in range(1, per_row)]
         home = jnp.stack(home, axis=0)
         mixed = jnp.einsum("rst,rsd->td", weights, home, preferred_element_type=F32).astype(BF)
-        outs.append(lax.psum_scatter(mixed, "dp", scatter_dimension=0, tiled=True))
+        outs.append(scatter_dp(mixed, 2 * n + 1))
     return jnp.concatenate(outs, axis=1)
 
 

time: 308 us -> 179 us (0.58)
  waiting for transfers between devices: 256 us -> 26.1 us
  Pallas kernels: 0 us -> 125 us
  between operations: 13.4 us -> 0.31 us
  matrix products: 19.5 us -> 14.8 us
    pallas_call x0 -> x4, Pallas kernels: none -> 125 us  [the longest x2 64 us: gather_dp(): pl.pallas_call(functools.partial(gather_kernel, ring), name='gather%d' %...]
    reduce_scatter x2 -> x0, waiting for transfers between devices: 116 us -> none  [on_device(): outs.append(lax.psum_scatter(mixed, 'dp', scatter_dimension=0, tiled=True))]
    all_gather x2 -> x0, waiting for transfers between devices: 96.9 us -> none  [the longest x1 53.8 us: on_device(): lax.all_gather(jnp.concatenate([tokens[:, :part], meta], axis=1), 'dp', a...]
    ppermute x4, waiting for transfers between devices: 35.1 us -> 22.3 us  [turn(): return lax.ppermute(block, 'expert', route)]
    ppermute x4, waiting for transfers between devices: 7.81 us -> 3.87 us  [swap_cores(): return lax.ppermute(block, 'expert', [(c, c ^ 1) for c in range(col_size)])]
  transfers between devices with their start and end apart: 12 -> 8, of which waited for: 10 -> 5; matrix products, arithmetic and copies ran while one was open for 5% -> 3% of each run, Pallas kernels for 0% -> 34%
where the time goes in v2:
time: 179 us
  Pallas kernels  125 us (70%)
  waiting for transfers between devices  26.1 us (15%)
  matrix products  14.8 us (8%)
  starting transfers between devices  4.64 us (3%)
  other arithmetic  4.42 us (2%)
  local copies, waits for them, and re-layouts  3.93 us (2%)
    pallas_call x2, Pallas kernels, gather_dp(): pl.pallas_call(functools.partial(gather_kernel, ring), name='gather%d' %...  64 us
    pallas_call x2, Pallas kernels, scatter_dp(): pl.pallas_call(functools.partial(scatter_kernel, ring), name='scatter%d'...  60.6 us
    ppermute x4, waiting for transfers between devices, turn(): return lax.ppermute(block, 'expert', route)  22.3 us
    dot_general x2, matrix products, on_device(): jnp.einsum('rst,td->rsd', spots, columns[n], preferred_element_type=F32)  4.34 us
    ppermute x4, waiting for transfers between devices, swap_cores(): return lax.ppermute(block, 'expert', [(c, c ^ 1) for c in range(col_size)])  3.87 us
    ppermute x4, starting transfers between devices, turn(): return lax.ppermute(block, 'expert', route)  3.85 us
  transfers between devices with their start and end apart: 8, of which 5 were waited for; matrix products, arithmetic and copies ran while one was open for 3% of the time, Pallas kernels for 34%

profile of v2, /device:TPU:0, one launch (start us, length us, event | category | flops | bytes accessed | tf_op | source)
XLA Modules:
  0.0 178.8 jit_solution(6027472870108152463)
XLA Ops:
  0.0 0.0 copy-start
  0.0 0.8 convert_bitcast_fusion.1
  0.8 0.7 convert_element_type.90
  1.5 0.7 convert_element_type.91
  2.2 0.1 copy.14
  2.3 0.1 copy.13
  2.4 1.1 fusion.49
  3.5 0.1 concatenate.23.src
  3.6 35.3 %gather0.1 = bf16[1024,1152]{1,0:T(8,128)(2,1)S(1)} custom-call(bf16[128,1152]{1,0:T(8,128)(2,1)S(1)} %concatenate.23.src), custom_call_target="tpu_custom_call" | custom-call | bytes 62914560 | tf_op jit(solution)/shard_map/gather0/pallas_call | solution.py:219
  38.9 0.0 copy-start.1
  38.9 1.4 copy-done.1
  40.3 0.1 slice.95
  40.4 0.1 fusion.50
  40.6 0.1 compare_convert_fusion
  40.7 0.2 copy.15
  40.8 0.2 copy.17
  41.0 0.1 multiply_reduce_fusion.1
  41.1 0.2 fusion.31
  41.3 0.1 multiply_reduce_fusion
  41.4 0.1 convert_bitcast_fusion
  41.5 0.1 copy.28
  41.6 3.0 %fusion.9 = bf16[2,256,1024]{2,1,0:T(8,128)(2,1)S(1)} fusion(bf16[1024,1152]{1,0:T(8,128)(2,1)} %copy-done.1, s32[2,1024]{1,0:T(2,128)S(1)} %bitcast.64), kind=kOutput, calls=%fused_computation.19 | convolution fusion | flops 1074790400 | bytes 3153920 | tf_op jit(solution)/shard_map/rst,td->rsd/dot_general | solution.py:332
  44.5 0.1 slice_bitcast_fusion.5
  44.6 1.6 collective-permute-start
  46.2 28.7 %gather2.1 = bf16[1024,1024]{1,0:T(8,128)(2,1)S(1)} custom-call(bf16[128,1024]{1,0:T(8,128)(2,1)S(1)} %get-tuple-element.19.src), custom_call_target="tpu_custom_call" | custom-call | bytes 62914560 | tf_op jit(solution)/shard_map/gather2/pallas_call | solution.py:219
  74.9 1.4 fusion.12
  76.3 0.1 slice_bitcast_fusion.3
  76.4 0.6 collective-permute-start.2
  77.0 0.0 collective-permute-done
  77.0 0.1 pad_maximum_fusion
  77.1 0.1 collective-permute-start.1
  77.1 10.1 %collective-permute-done.2 = bf16[256,1024]{1,0:T(8,128)(2,1)S(1)} collective-permute-done((bf16[256,1024]{1,0:T(8,128)(2,1)S(1)}, bf16[256,1024]{1,0:T(8,128)(2,1)S(1)}, u32[]{:S(2)}, u32[]{:S(2)}) %collective-permute-start.2) | collective-permute-done | bytes 524320 | tf_op jit(solution)/shard_map/ppermute | solution.py:266
  87.2 0.1 pad_maximum_fusion.1
  87.3 0.0 copy-start.2
  87.3 0.1 collective-permute-start.3
  87.4 0.0 collective-permute-done.1
  87.4 2.6 %collective-permute-done.3 = bf16[512,1024]{1,0:T(8,128)(2,1)S(1)} collective-permute-done((bf16[512,1024]{1,0:T(8,128)(2,1)S(1)}, bf16[512,1024]{1,0:T(8,128)(2,1)S(1)}, u32[]{:S(2)}, u32[]{:S(2)}) %collective-permute-start.3) | collective-permute-done | bytes 1048608 | tf_op jit(solution)/shard_map/ppermute | solution.py:261
  90.0 0.0 copy-done
  90.0 2.3 %fusion.7 = f32[1024,384]{1,0:T(8,128)S(1)} fusion(bf16[1,2048,384]{2,1,0:T(8,128)(2,1)S(1)} %copy-done, bf16[512,1024]{1,0:T(8,128)(2,1)S(1)} %collective-permute-done.3, bf16[256,1024]{1,0:T(8,128)(2,1)S(1)} %collective-permute-done.2, bf16[256,1024]{1,0:T(8,128)(2,1)S(1)} %get-tuple-element.16, bf16[512,1024]{1,0:T(8,128)(2,1)S(1)} %collective-permute-done.1, ...), kind=kOutput, calls=%fused_computation.16 | convolution fusion | flops 1635778560 | bytes 7340032 | tf_op jit(solution)/shard_map/dot_general | solution.py:337
  92.3 0.0 copy-done.2
  92.4 0.0 copy-start.3
  92.4 2.4 %multiply_convert_fusion = bf16[1024,384]{1,0:T(8,128)(2,1)S(1)} fusion(f32[1024,384]{1,0:T(8,128)S(1)} %fusion.7, bf16[1,2048,384]{2,1,0:T(8,128)(2,1)S(1)} %copy-done.2, bf16[512,1024]{1,0:T(8,128)(2,1)S(1)} %collective-permute-done.3, bf16[256,1024]{1,0:T(8,128)(2,1)S(1)} %collective-permute-done.2, bf16[256,1024]{1,0:T(8,128)(2,1)S(1)} %get-tuple-element.16, ...), kind=kOutput, calls=%fused_computation.18 | convolution fusion | flops 1638137856 | bytes 8126464 | tf_op jit(solution)/shard_map/dot_general | solution.py:338
  94.8 0.0 copy-done.3
  94.8 1.2 convolution_convert_fusion
  96.1 0.1 slice.108
  96.1 0.2 collective-permute-start.6
  96.3 1.2 convolution_convert_fusion.1
  97.6 0.1 slice.103
  97.7 0.4 collective-permute-start.4
  98.1 0.8 collective-permute-done.6
  98.9 0.4 add_convert_fusion
  99.3 0.1 slice_bitcast_fusion
  99.4 0.6 collective-permute-start.7
  99.9 0.5 collective-permute-done.4
  100.4 0.4 add_convert_fusion.1
  100.8 0.1 slice_bitcast_fusion.1
  100.9 1.1 collective-permute-start.5
  102.0 12.2 %collective-permute-done.7 = bf16[256,1024]{1,0:T(8,128)(2,1)S(1)} collective-permute-done((bf16[256,1024]{1,0:T(8,128)(2,1)S(1)}, bf16[256,1024]{1,0:T(8,128)(2,1)S(1)}, u32[]{:S(2)}, u32[]{:S(2)}) %collective-permute-start.7) | collective-permute-done | bytes 524320 | tf_op jit(solution)/shard_map/ppermute | solution.py:266
  114.2 1.5 bitcast_convert_fusion.part
  115.8 32.1 %scatter3.1 = bf16[128,1024]{1,0:T(8,128)(2,1)S(1)} custom-call(bf16[1024,1024]{1,0:T(8,128)(2,1)S(1)} %bitcast_convert_fusion.part), custom_call_target="tpu_custom_call" | custom-call | bytes 62914560 | tf_op jit(solution)/shard_map/scatter3/pallas_call | solution.py:241
  147.9 0.0 collective-permute-done.5
  147.9 1.6 bitcast_convert_fusion.1.part
  149.4 28.6 %scatter1.1 = bf16[128,1024]{1,0:T(8,128)(2,1)S(1)} custom-call(bf16[1024,1024]{1,0:T(8,128)(2,1)S(1)} %bitcast_convert_fusion.1.part), custom_call_target="tpu_custom_call" | custom-call | bytes 62914560 | tf_op jit(solution)/shard_map/scatter1/pallas_call | solution.py:241
  178.0 0.8 pad_maximum_fusion.2
  (7 shorter events, 0.1 us)
Async XLA Ops:
  0.0 90.0 %copy-start = (bf16[1,2048,384]{2,1,0:T(8,128)(2,1)S(1)}, bf16[1,2048,384]{2,1,0:T(8,128)(2,1)}, u32[]{:S(2)}) copy-start(bf16[1,2048,384]{2,1,0:T(8,128)(2,1)} %param.11) | copy-start | bytes 4718596
  38.9 1.4 copy-start.1
  44.6 32.4 %collective-permute-start = (bf16[256,1024]{1,0:T(8,128)(2,1)S(1)}, bf16[256,1024]{1,0:T(8,128)(2,1)S(1)}, u32[]{:S(2)}, u32[]{:S(2)}) collective-permute-start(bf16[256,1024]{1,0:T(8,128)(2,1)S(1)} %get-tuple-element.15), channel_id=1, source_target_pairs={{0,2},{1,3},{2,0},{3,1},{4,6},{5,7},{6,4},{7,5},{8,10},{9,11},{10,... | collective-permute-start | bytes 1572872 | tf_op jit(solution)/shard_map/ppermute | solution.py:266
  76.4 10.8 %collective-permute-start.2 = (bf16[256,1024]{1,0:T(8,128)(2,1)S(1)}, bf16[256,1024]{1,0:T(8,128)(2,1)S(1)}, u32[]{:S(2)}, u32[]{:S(2)}) collective-permute-start(bf16[256,1024]{1,0:T(8,128)(2,1)S(1)} %get-tuple-element.17), channel_id=1, source_target_pairs={{0,2},{1,3},{2,0},{3,1},{4,6},{5,7},{6,4},{7,5},{8,10},{9,11},{10,... | collective-permute-start | bytes 1572872 | tf_op jit(solution)/shard_map/ppermute | solution.py:266
  77.1 10.3 %collective-permute-start.1 = (bf16[512,1024]{1,0:T(8,128)(2,1)S(1)}, bf16[512,1024]{1,0:T(8,128)(2,1)S(1)}, u32[]{:S(2)}, u32[]{:S(2)}) collective-permute-start(bf16[512,1024]{1,0:T(8,128)(2,1)S(1)} %pad_maximum_fusion), channel_id=1, source_target_pairs={{0,1},{1,0},{2,3},{3,2},{4,5},{5,4},{6,7},{7,6},{8,9},{9,8},{10,11... | collective-permute-start | bytes 3145736 | tf_op jit(solution)/shard_map/ppermute | solution.py:261
  87.3 5.1 %copy-start.2 = (bf16[1,2048,384]{2,1,0:T(8,128)(2,1)S(1)}, bf16[1,2048,384]{2,1,0:T(8,128)(2,1)}, u32[]{:S(2)}) copy-start(bf16[1,2048,384]{2,1,0:T(8,128)(2,1)} %param.12) | copy-start | bytes 4718596
  87.3 2.7 %collective-permute-start.3 = (bf16[512,1024]{1,0:T(8,128)(2,1)S(1)}, bf16[512,1024]{1,0:T(8,128)(2,1)S(1)}, u32[]{:S(2)}, u32[]{:S(2)}) collective-permute-start(bf16[512,1024]{1,0:T(8,128)(2,1)S(1)} %pad_maximum_fusion.1), channel_id=1, source_target_pairs={{0,1},{1,0},{2,3},{3,2},{4,5},{5,4},{6,7},{7,6},{8,9},{9,8},{10,11... | collective-permute-start | bytes 3145736 | tf_op jit(solution)/shard_map/ppermute | solution.py:261
  92.4 2.4 %copy-start.3 = (bf16[1,384,2048]{2,1,0:T(8,128)(2,1)S(1)}, bf16[1,384,2048]{2,1,0:T(8,128)(2,1)}, u32[]{:S(2)}) copy-start(bf16[1,384,2048]{2,1,0:T(8,128)(2,1)} %param.13) | copy-start | bytes 4718596
  96.1 2.7 %collective-permute-start.6 = (bf16[512,1024]{1,0:T(8,128)(2,1)S(1)}, bf16[512,1024]{1,0:T(8,128)(2,1)S(1)}, u32[]{:S(2)}, u32[]{:S(2)}) collective-permute-start(bf16[512,1024]{1,0:T(8,128)(2,1)S(1)} %slice.108), channel_id=1, source_target_pairs={{0,1},{1,0},{2,3},{3,2},{4,5},{5,4},{6,7},{7,6},{8,9},{9,8},{10,11... | collective-permute-start | bytes 3145736 | tf_op jit(solution)/shard_map/ppermute | solution.py:261
  97.7 2.7 %collective-permute-start.4 = (bf16[512,1024]{1,0:T(8,128)(2,1)S(1)}, bf16[512,1024]{1,0:T(8,128)(2,1)S(1)}, u32[]{:S(2)}, u32[]{:S(2)}) collective-permute-start(bf16[512,1024]{1,0:T(8,128)(2,1)S(1)} %slice.103), channel_id=1, source_target_pairs={{0,1},{1,0},{2,3},{3,2},{4,5},{5,4},{6,7},{7,6},{8,9},{9,8},{10,11... | collective-permute-start | bytes 3145736 | tf_op jit(solution)/shard_map/ppermute | solution.py:261
  99.4 14.9 %collective-permute-start.7 = (bf16[256,1024]{1,0:T(8,128)(2,1)S(1)}, bf16[256,1024]{1,0:T(8,128)(2,1)S(1)}, u32[]{:S(2)}, u32[]{:S(2)}) collective-permute-start(bf16[256,1024]{1,0:T(8,128)(2,1)S(1)} %get-tuple-element.13), channel_id=1, source_target_pairs={{0,2},{1,3},{2,0},{3,1},{4,6},{5,7},{6,4},{7,5},{8,10},{9,11},{10,... | collective-permute-start | bytes 1572872 | tf_op jit(solution)/shard_map/ppermute | solution.py:266
  100.9 47.0 %collective-permute-start.5 = (bf16[256,1024]{1,0:T(8,128)(2,1)S(1)}, bf16[256,1024]{1,0:T(8,128)(2,1)S(1)}, u32[]{:S(2)}, u32[]{:S(2)}) collective-permute-start(bf16[256,1024]{1,0:T(8,128)(2,1)S(1)} %get-tuple-element.11), channel_id=1, source_target_pairs={{0,2},{1,3},{2,0},{3,1},{4,6},{5,7},{6,4},{7,5},{8,10},{9,11},{10,... | collective-permute-start | bytes 1572872 | tf_op jit(solution)/shard_map/ppermute | solution.py:266

commit v3 on v2

--- a/solution.py
+++ b/solution.py
@@ -9,7 +9,7 @@
 
 BF = jnp.bfloat16
 F32 = jnp.float32
-CHUNKS = 2
+SIXTEENTHS = (8, 5, 3)
 
 
 class Wires:
@@ -53,6 +53,11 @@
     return z, x, ahead, behind, z * 2 + 1 - x
 
 
+def pieces(rows):
+    unit = rows // 8
+    return [(0, 3 * unit), (3 * unit, 3 * unit), (6 * unit, unit), (7 * unit, unit)]
+
+
 def greet(peers):
     barrier = pltpu.get_barrier_semaphore()
     for peer in peers:
@@ -66,18 +71,19 @@
     z, x, ahead, behind, other = places(ring)
     greet((ahead, behind, other))
     rows = src.shape[0]
-    piece = rows // 4
+    spans = pieces(rows)
     wires = Wires(ssem, rsem)
     to = [ahead, behind]
 
     def at(zz, xx, k):
-        start = pl.multiple_of((zz * 2 + xx) * rows + k * piece, piece)
-        return out.at[pl.ds(start, piece)]
+        begin, count = spans[k]
+        start = pl.multiple_of((zz * 2 + xx) * rows + begin, rows // 8)
+        return out.at[pl.ds(start, count)]
 
     def back(k, s):
         return lax.rem(z + (ring - s if k % 2 == 0 else s), ring)
 
-    own = [src.at[pl.ds(k * piece, piece)] for k in range(4)]
+    own = [src.at[pl.ds(*spans[k])] for k in range(4)]
     ring_lane = {}
     for k in range(4):
         for s in range(ring - 1):
@@ -127,13 +133,14 @@
     z, x, ahead, behind, other = places(ring)
     greet((ahead, behind, other))
     rows = out.shape[0]
-    piece = rows // 4
+    spans = pieces(rows)
     wires = Wires(ssem, rsem)
     to = [ahead, behind]
 
     def at(zz, xx, k):
-        start = pl.multiple_of((zz * 2 + xx) * rows + k * piece, piece)
-        return part.at[pl.ds(start, piece)]
+        begin, count = spans[k]
+        start = pl.multiple_of((zz * 2 + xx) * rows + begin, rows // 8)
+        return part.at[pl.ds(start, count)]
 
     def goal(k, s):
         return lax.rem(z + (ring - 1 - s if k % 2 == 0 else 1 + s), ring)
@@ -192,14 +199,14 @@
     for k in (0, 1):
         wires.arrive(cross_a.at[k, ring - 1], lanes["c", k, ring - 1], other)
         wires.arrive(ring_a.at[k, ring - 2], lanes[k, 0, ring - 2], other)
-        out[pl.ds(k * piece, piece)] = total(
+        out[pl.ds(*spans[k])] = total(
             at(z, x, k), cross_a.at[k, ring - 1], ring_a.at[k, ring - 2]
         )
     for k in (2, 3):
         came = ring_b.at[k - 2, 0, ring - 2]
         wires.arrive(came, lanes[k, 0, ring - 2], other)
         wires.arrive(cross_b.at[k - 2], lanes["c", k, 0], other)
-        out[pl.ds(k * piece, piece)] = total(at(z, x, k), came, cross_b.at[k - 2])
+        out[pl.ds(*spans[k])] = total(at(z, x, k), came, cross_b.at[k - 2])
     wires.finish()
 
 
@@ -236,7 +243,7 @@
     dp_size = lax.axis_size("dp")
     ring = dp_size // 2
     rows, wide = parts.shape[0] // dp_size, parts.shape[1]
-    piece = rows // 4
+    (_, long), (_, short) = pieces(rows)[1:3]
     count = 8 * ring - 4
     return pl.pallas_call(
         functools.partial(scatter_kernel, ring),
@@ -245,10 +252,10 @@
         in_specs=[VM],
         out_specs=VM,
         scratch_shapes=[
-            pltpu.VMEM((2, ring, piece, wide), BF),
-            pltpu.VMEM((2, ring - 1, piece, wide), BF),
-            pltpu.VMEM((2, 2, ring - 1, piece, wide), BF),
-            pltpu.VMEM((2, piece, wide), BF),
+            pltpu.VMEM((2, ring, long, wide), BF),
+            pltpu.VMEM((2, ring - 1, long, wide), BF),
+            pltpu.VMEM((2, 2, ring - 1, short, wide), BF),
+            pltpu.VMEM((2, short, wide), BF),
             pltpu.SemaphoreType.DMA((count,)),
             pltpu.SemaphoreType.DMA((count,)),
         ],
@@ -301,7 +308,11 @@
     per_row = col_size // 2
     capacity = tok_rows * top // experts
     col_cap = dp_size * capacity // 2
-    part = width // CHUNKS
+    bounds = [0]
+    for share in SIXTEENTHS:
+        bounds.append(bounds[-1] + width * share // 16)
+    spans = list(zip(bounds[:-1], bounds[1:]))
+    part = bounds[1]
 
     used = 2 * top + experts
     meta = jnp.concatenate(
@@ -314,9 +325,12 @@
         axis=1,
     )
     first = gather_dp(jnp.concatenate([tokens[:, :part], meta], axis=1), 0)
-    columns = [first[:, :part]]
-    for n in range(1, CHUNKS):
-        columns.append(gather_dp(tokens[:, n * part : (n + 1) * part], 2 * n))
+    columns = [first]
+    for n, (low, high) in enumerate(spans[1:], 1):
+        block, columns[-1] = lax.optimization_barrier((tokens[:, low:high], columns[-1]))
+        columns.append(gather_dp(block, 2 * n))
+    first = columns[0]
+    columns[0] = first[:, :part]
     info = first[:, part:].reshape(dp_size, tok_rows, -1).astype(F32)
     spots, weights = slot_matrices(
         info[:, :, :top],
@@ -328,7 +342,7 @@
 
     gate_half, up_half, down_half = gate_proj[0], up_proj[0], down_proj[0]
     stacks = []
-    for n in range(CHUNKS):
+    for n in range(len(spans)):
         slots = jnp.einsum("rst,td->rsd", spots, columns[n], preferred_element_type=F32).astype(BF)
         held = [slots[0]] + [turn(slots[r], col_size, r) for r in range(1, per_row)]
         held = jnp.concatenate(held, axis=0)
@@ -339,19 +353,23 @@
     hidden = (jax.nn.silu(gate_val) * up_val).astype(BF)
 
     own = per_row * col_cap
-    outs = []
-    for n in range(CHUNKS):
-        partial = jnp.dot(
-            hidden, down_half[:, n * part : (n + 1) * part], preferred_element_type=F32
-        ).astype(BF)
+    homes = []
+    for low, high in spans[::-1]:
+        partial = jnp.dot(hidden, down_half[:, low:high], preferred_element_type=F32).astype(BF)
         back = swap_cores(partial[own:], col_size)
         merged = (partial[:own].astype(F32) + back.astype(F32)).astype(BF)
-        merged = merged.reshape(per_row, col_cap, part)
+        if not homes:
+            hidden, merged = lax.optimization_barrier((hidden, merged))
+        merged = merged.reshape(per_row, col_cap, high - low)
         home = [merged[0]] + [turn(merged[r], col_size, -r) for r in range(1, per_row)]
-        home = jnp.stack(home, axis=0)
+        homes.append(jnp.stack(home, axis=0))
+    outs = []
+    for n, home in enumerate(homes):
+        if outs:
+            home, outs[-1] = lax.optimization_barrier((home, outs[-1]))
         mixed = jnp.einsum("rst,rsd->td", weights, home, preferred_element_type=F32).astype(BF)
         outs.append(scatter_dp(mixed, 2 * n + 1))
-    return jnp.concatenate(outs, axis=1)
+    return jnp.concatenate(outs[::-1], axis=1)
 
 
 def solution(mesh):

time: 179 us -> 206 us (1.15)
  other arithmetic: 4.42 us -> 23.2 us
  waiting for transfers between devices: 26.1 us -> 12.1 us
  Pallas kernels: 125 us -> 139 us
  starting transfers between devices: 4.64 us -> 8.78 us
  matrix products: 14.8 us -> 17.1 us
    concatenate x1 -> x2, other arithmetic: 0.83 us -> 19.7 us  [the longest x1 18.8 us: on_device(): rows = jnp.concatenate(stacks, axis=1)]
    ppermute x4 -> x6, waiting for transfers between devices: 22.3 us -> 8.79 us  [turn(): return lax.ppermute(block, 'expert', route)]
    pallas_call x2 -> x3, Pallas kernels: 60.6 us -> 69.4 us  [scatter_dp(): pl.pallas_call(functools.partial(scatter_kernel, ring), name='scatter%d'...]
    pallas_call x2 -> x3, Pallas kernels: 64 us -> 69.1 us  [gather_dp(): pl.pallas_call(functools.partial(gather_kernel, ring), name='gather%d' %...]
    ppermute x4 -> x6, starting transfers between devices: 3.85 us -> 7.51 us  [turn(): return lax.ppermute(block, 'expert', route)]
    dot_general x2 -> x3, matrix products: 4.34 us -> 5.42 us  [on_device(): jnp.einsum('rst,td->rsd', spots, columns[n], preferred_element_type=F32)]
  transfers between devices with their start and end apart: 8 -> 12, of which waited for: 5 -> 4; matrix products, arithmetic and copies ran while one was open for 3% -> 4% of each run, Pallas kernels for 34% -> 40%
where the time goes in v3:
time: 206 us
  Pallas kernels  139 us (67%)
  other arithmetic  23.2 us (11%)
  matrix products  17.1 us (8%)
  waiting for transfers between devices  12.1 us (6%)
  starting transfers between devices  8.78 us (4%)
  local copies, waits for them, and re-layouts  5.86 us (3%)
    pallas_call x3, Pallas kernels, scatter_dp(): pl.pallas_call(functools.partial(scatter_kernel, ring), name='scatter%d'...  69.4 us
    pallas_call x3, Pallas kernels, gather_dp(): pl.pallas_call(functools.partial(gather_kernel, ring), name='gather%d' %...  69.1 us
    concatenate x1, other arithmetic, on_device(): rows = jnp.concatenate(stacks, axis=1)  18.8 us
    ppermute x6, waiting for transfers between devices, turn(): return lax.ppermute(block, 'expert', route)  8.79 us
    ppermute x6, starting transfers between devices, turn(): return lax.ppermute(block, 'expert', route)  7.51 us
    dot_general x3, matrix products, on_device(): jnp.einsum('rst,td->rsd', spots, columns[n], preferred_element_type=F32)  5.42 us
  transfers between devices with their start and end apart: 12, of which 4 were waited for; matrix products, arithmetic and copies ran while one was open for 4% of the time, Pallas kernels for 40%

profile of v3, /device:TPU:0, one launch (start us, length us, event | category | flops | bytes accessed | tf_op | source)
XLA Modules:
  0.0 206.1 jit_solution(6942879941125174935)
XLA Ops:
  0.0 1.0 slice.99.src
  1.1 1.0 slice.100
  2.0 0.7 convert_bitcast_fusion.1
  2.7 0.7 convert_element_type.108
  3.4 0.7 convert_element_type.109
  4.1 0.1 copy.15
  4.2 0.1 copy.14
  4.3 0.1 concatenate.30.src
  4.5 31.7 %gather0.1 = bf16[1024,1152]{1,0:T(8,128)(2,1)S(1)} custom-call(bf16[128,1152]{1,0:T(8,128)(2,1)S(1)} %concatenate.30.src), custom_call_target="tpu_custom_call" | custom-call | bytes 62914560 | tf_op jit(solution)/shard_map/gather0/pallas_call | solution.py:226
  36.2 1.4 copy-done.1
  37.6 0.1 slice.132
  37.7 0.1 fusion.51
  37.9 0.1 compare_convert_fusion
  38.0 0.2 copy.16
  38.1 0.2 copy.18
  38.3 0.1 multiply_reduce_fusion.1
  38.4 0.2 fusion.35
  38.6 0.1 multiply_reduce_fusion
  38.7 0.1 convert_bitcast_fusion
  38.9 3.0 %fusion.10 = bf16[2,256,1024]{2,1,0:T(8,128)(2,1)S(1)} fusion(bf16[1024,1152]{1,0:T(8,128)(2,1)} %copy-done.1, s32[2,1024]{1,0:T(2,128)S(1)} %bitcast.84), kind=kOutput, calls=%fused_computation.20 | convolution fusion | flops 1074790400 | bytes 3153920 | tf_op jit(solution)/shard_map/rst,td->rsd/dot_general | solution.py:346
  41.8 0.1 slice_bitcast_fusion.2
  41.9 1.6 collective-permute-start
  43.5 0.9 slice.108.src
  44.4 20.5 %gather2.1 = bf16[1024,640]{1,0:T(8,128)(2,1)S(1)} custom-call(bf16[128,640]{1,0:T(8,128)(2,1)S(1)} %slice.99.src), custom_call_target="tpu_custom_call" | custom-call | bytes 62914560 | tf_op jit(solution)/shard_map/gather2/pallas_call | solution.py:226
  64.9 1.3 fusion.13
  66.2 0.1 slice_bitcast_fusion.5
  66.2 0.6 collective-permute-start.2
  66.8 16.9 %gather4.1 = bf16[1024,384]{1,0:T(8,128)(2,1)S(1)} custom-call(bf16[128,384]{1,0:T(8,128)(2,1)S(1)} %slice.108.src), custom_call_target="tpu_custom_call" | custom-call | bytes 62914560 | tf_op jit(solution)/shard_map/gather4/pallas_call | solution.py:226
  83.8 0.1 pad_maximum_fusion
  83.9 0.1 collective-permute-start.1
  83.9 1.2 fusion.15
  85.2 1.6 collective-permute-start.4
  86.8 0.3 collective-permute-start.3
  87.1 5.4 %collective-permute-done.4 = bf16[256,384]{1,0:T(8,128)(2,1)S(1)} collective-permute-done((bf16[256,384]{1,0:T(8,128)(2,1)S(1)}, bf16[256,384]{1,0:T(8,128)(2,1)S(1)}, u32[]{:S(2)}, u32[]{:S(2)}) %collective-permute-start.4) | collective-permute-done | bytes 196640 | tf_op jit(solution)/shard_map/ppermute | solution.py:273
  92.6 0.1 collective-permute-start.5
  92.6 1.7 collective-permute-done.5
  94.4 18.8 %maximum_maximum_fusion = bf16[1024,2048]{1,0:T(8,128)(2,1)S(1)} fusion(bf16[512,384]{1,0:T(8,128)(2,1)S(1)} %collective-permute-done.5, bf16[256,384]{1,0:T(8,128)(2,1)S(1)} %collective-permute-done.4, bf16[256,384]{1,0:T(8,128)(2,1)S(1)} %get-tuple-element.40, bf16[512,640]{1,0:T(8,128)(2,1)S(1)} %collective-permute-done.3, ...), kind=kLoop, calls=%fused_computation | loop fusion | flops 37748736 | bytes 8388608 | tf_op jit(solution)/shard_map/concatenate | solution.py:350
  113.2 2.3 %fusion.8 = f32[1024,384]{1,0:T(8,128)S(1)} fusion(bf16[1024,2048]{1,0:T(8,128)(2,1)S(1)} %maximum_maximum_fusion, bf16[1,2048,384]{2,1,0:T(8,128)(2,1)S(1)} %copy-done), kind=kOutput, calls=%fused_computation.17 | convolution fusion | flops 1610612736 | bytes 7340032 | tf_op jit(solution)/shard_map/dot_general | solution.py:351
  115.6 2.4 %multiply_convert_fusion = bf16[1024,384]{1,0:T(8,128)(2,1)S(1)} fusion(f32[1024,384]{1,0:T(8,128)S(1)} %fusion.8, bf16[1024,2048]{1,0:T(8,128)(2,1)S(1)} %maximum_maximum_fusion, bf16[1,2048,384]{2,1,0:T(8,128)(2,1)S(1)} %copy-done.3), kind=kOutput, calls=%fused_computation.19 | convolution fusion | flops 1612972032 | bytes 8126464 | tf_op jit(solution)/shard_map/dot_general | solution.py:352
  118.0 0.6 convolution_convert_fusion.2
  118.7 0.2 collective-permute-start.6
  118.9 1.6 collective-permute-done.6
  120.5 0.1 add_convert_fusion.2
  120.6 0.9 convolution_convert_fusion.1
  121.6 0.2 collective-permute-start.9
  121.8 1.2 convolution_convert_fusion
  123.1 0.1 slice.145
  123.1 0.4 collective-permute-start.7
  123.6 1.6 collective-permute-start.11
  125.2 0.2 add_convert_fusion.1
  125.4 0.6 collective-permute-start.10
  126.0 0.4 add_convert_fusion
  126.4 0.1 slice_bitcast_fusion
  126.5 1.6 collective-permute-start.8
  128.1 3.4 %collective-permute-done.11 = bf16[256,384]{1,0:T(8,128)(2,1)S(1)} collective-permute-done((bf16[256,384]{1,0:T(8,128)(2,1)S(1)}, bf16[256,384]{1,0:T(8,128)(2,1)S(1)}, u32[]{:S(2)}, u32[]{:S(2)}) %collective-permute-start.11) | collective-permute-done | bytes 196640 | tf_op jit(solution)/shard_map/ppermute | solution.py:273
  131.5 1.0 bitcast_convert_fusion.2.part
  132.5 21.6 %scatter1.1 = bf16[128,384]{1,0:T(8,128)(2,1)S(1)} custom-call(bf16[1024,384]{1,0:T(8,128)(2,1)S(1)} %bitcast_convert_fusion.2.part), custom_call_target="tpu_custom_call" | custom-call | bytes 62914560 | tf_op jit(solution)/shard_map/scatter1/pallas_call | solution.py:248
  154.1 0.1 pad_maximum_fusion.3
  154.2 1.5 bitcast_convert_fusion.1.part
  155.7 22.6 %scatter3.1 = bf16[128,640]{1,0:T(8,128)(2,1)S(1)} custom-call(bf16[1024,640]{1,0:T(8,128)(2,1)S(1)} %bitcast_convert_fusion.1.part), custom_call_target="tpu_custom_call" | custom-call | bytes 62914560 | tf_op jit(solution)/shard_map/scatter3/pallas_call | solution.py:248
  178.3 0.1 pad_maximum_fusion.1
  178.5 1.6 bitcast_convert_fusion.part
  180.0 25.2 %scatter5.1 = bf16[128,1024]{1,0:T(8,128)(2,1)S(1)} custom-call(bf16[1024,1024]{1,0:T(8,128)(2,1)S(1)} %bitcast_convert_fusion.part), custom_call_target="tpu_custom_call" | custom-call | bytes 62914560 | tf_op jit(solution)/shard_map/scatter5/pallas_call | solution.py:248
  205.2 0.8 pad_maximum_fusion.4
  (30 shorter events, 0.5 us)
Async XLA Ops:
  0.0 113.2 %copy-start = (bf16[1,2048,384]{2,1,0:T(8,128)(2,1)S(1)}, bf16[1,2048,384]{2,1,0:T(8,128)(2,1)}, u32[]{:S(2)}) copy-start(bf16[1,2048,384]{2,1,0:T(8,128)(2,1)} %param.11) | copy-start | bytes 4718596
  36.2 1.4 copy-start.1
  41.9 41.9 %collective-permute-start = (bf16[256,1024]{1,0:T(8,128)(2,1)S(1)}, bf16[256,1024]{1,0:T(8,128)(2,1)S(1)}, u32[]{:S(2)}, u32[]{:S(2)}) collective-permute-start(bf16[256,1024]{1,0:T(8,128)(2,1)S(1)} %get-tuple-element.33), channel_id=1, source_target_pairs={{0,2},{1,3},{2,0},{3,1},{4,6},{5,7},{6,4},{7,5},{8,10},{9,11},{10,... | collective-permute-start | bytes 1572872 | tf_op jit(solution)/shard_map/ppermute | solution.py:273
  66.2 20.5 %collective-permute-start.2 = (bf16[256,640]{1,0:T(8,128)(2,1)S(1)}, bf16[256,640]{1,0:T(8,128)(2,1)S(1)}, u32[]{:S(2)}, u32[]{:S(2)}) collective-permute-start(bf16[256,640]{1,0:T(8,128)(2,1)S(1)} %get-tuple-element.37), channel_id=1, source_target_pairs={{0,2},{1,3},{2,0},{3,1},{4,6},{5,7},{6,4},{7,5},{8,10},{9,11},{10,... | collective-permute-start | bytes 983048 | tf_op jit(solution)/shard_map/ppermute | solution.py:273
  83.9 10.5 %collective-permute-start.1 = (bf16[512,1024]{1,0:T(8,128)(2,1)S(1)}, bf16[512,1024]{1,0:T(8,128)(2,1)S(1)}, u32[]{:S(2)}, u32[]{:S(2)}) collective-permute-start(bf16[512,1024]{1,0:T(8,128)(2,1)S(1)} %pad_maximum_fusion), channel_id=1, source_target_pairs={{0,1},{1,0},{2,3},{3,2},{4,5},{5,4},{6,7},{7,6},{8,9},{9,8},{10,11... | collective-permute-start | bytes 3145736 | tf_op jit(solution)/shard_map/ppermute | solution.py:268
  85.2 7.4 %collective-permute-start.4 = (bf16[256,384]{1,0:T(8,128)(2,1)S(1)}, bf16[256,384]{1,0:T(8,128)(2,1)S(1)}, u32[]{:S(2)}, u32[]{:S(2)}) collective-permute-start(bf16[256,384]{1,0:T(8,128)(2,1)S(1)} %get-tuple-element.41), channel_id=1, source_target_pairs={{0,2},{1,3},{2,0},{3,1},{4,6},{5,7},{6,4},{7,5},{8,10},{9,11},{10,... | collective-permute-start | bytes 589832 | tf_op jit(solution)/shard_map/ppermute | solution.py:273
  86.8 7.5 %collective-permute-start.3 = (bf16[512,640]{1,0:T(8,128)(2,1)S(1)}, bf16[512,640]{1,0:T(8,128)(2,1)S(1)}, u32[]{:S(2)}, u32[]{:S(2)}) collective-permute-start(bf16[512,640]{1,0:T(8,128)(2,1)S(1)} %pad_maximum_fusion.2), channel_id=1, source_target_pairs={{0,1},{1,0},{2,3},{3,2},{4,5},{5,4},{6,7},{7,6},{8,9},{9,8},{10,11... | collective-permute-start | bytes 1966088 | tf_op jit(solution)/shard_map/ppermute | solution.py:268
  92.6 1.8 collective-permute-start.5
  113.2 2.3 %copy-start.3 = (bf16[1,2048,384]{2,1,0:T(8,128)(2,1)S(1)}, bf16[1,2048,384]{2,1,0:T(8,128)(2,1)}, u32[]{:S(2)}) copy-start(bf16[1,2048,384]{2,1,0:T(8,128)(2,1)} %param.12) | copy-start | bytes 4718596
  115.6 2.5 %copy-start.2 = (bf16[1,384,2048]{2,1,0:T(8,128)(2,1)S(1)}, bf16[1,384,2048]{2,1,0:T(8,128)(2,1)}, u32[]{:S(2)}) copy-start(bf16[1,384,2048]{2,1,0:T(8,128)(2,1)} %param.13) | copy-start | bytes 4718596
  118.7 1.8 collective-permute-start.6
  121.6 3.6 %collective-permute-start.9 = (bf16[512,640]{1,0:T(8,128)(2,1)S(1)}, bf16[512,640]{1,0:T(8,128)(2,1)S(1)}, u32[]{:S(2)}, u32[]{:S(2)}) collective-permute-start(bf16[512,640]{1,0:T(8,128)(2,1)S(1)} %slice.150), channel_id=1, source_target_pairs={{0,1},{1,0},{2,3},{3,2},{4,5},{5,4},{6,7},{7,6},{8,9},{9,8},{10,11... | collective-permute-start | bytes 1966088 | tf_op jit(solution)/shard_map/ppermute | solution.py:268
  123.1 2.9 %collective-permute-start.7 = (bf16[512,1024]{1,0:T(8,128)(2,1)S(1)}, bf16[512,1024]{1,0:T(8,128)(2,1)S(1)}, u32[]{:S(2)}, u32[]{:S(2)}) collective-permute-start(bf16[512,1024]{1,0:T(8,128)(2,1)S(1)} %slice.145), channel_id=1, source_target_pairs={{0,1},{1,0},{2,3},{3,2},{4,5},{5,4},{6,7},{7,6},{8,9},{9,8},{10,11... | collective-permute-start | bytes 3145736 | tf_op jit(solution)/shard_map/ppermute | solution.py:268
  123.6 7.8 %collective-permute-start.11 = (bf16[256,384]{1,0:T(8,128)(2,1)S(1)}, bf16[256,384]{1,0:T(8,128)(2,1)S(1)}, u32[]{:S(2)}, u32[]{:S(2)}) collective-permute-start(bf16[256,384]{1,0:T(8,128)(2,1)S(1)} %get-tuple-element.39), channel_id=1, source_target_pairs={{0,2},{1,3},{2,0},{3,1},{4,6},{5,7},{6,4},{7,5},{8,10},{9,11},{10,... | collective-permute-start | bytes 589832 | tf_op jit(solution)/shard_map/ppermute | solution.py:273
  125.4 28.6 %collective-permute-start.10 = (bf16[256,640]{1,0:T(8,128)(2,1)S(1)}, bf16[256,640]{1,0:T(8,128)(2,1)S(1)}, u32[]{:S(2)}, u32[]{:S(2)}) collective-permute-start(bf16[256,640]{1,0:T(8,128)(2,1)S(1)} %get-tuple-element.35), channel_id=1, source_target_pairs={{0,2},{1,3},{2,0},{3,1},{4,6},{5,7},{6,4},{7,5},{8,10},{9,11},{10,... | collective-permute-start | bytes 983048 | tf_op jit(solution)/shard_map/ppermute | solution.py:273
  126.5 51.8 %collective-permute-start.8 = (bf16[256,1024]{1,0:T(8,128)(2,1)S(1)}, bf16[256,1024]{1,0:T(8,128)(2,1)S(1)}, u32[]{:S(2)}, u32[]{:S(2)}) collective-permute-start(bf16[256,1024]{1,0:T(8,128)(2,1)S(1)} %get-tuple-element.31), channel_id=1, source_target_pairs={{0,2},{1,3},{2,0},{3,1},{4,6},{5,7},{6,4},{7,5},{8,10},{9,11},{10,... | collective-permute-start | bytes 1572872 | tf_op jit(solution)/shard_map/ppermute | solution.py:273

commit v4 on v3

--- a/solution.py
+++ b/solution.py
@@ -9,7 +9,7 @@
 
 BF = jnp.bfloat16
 F32 = jnp.float32
-SIXTEENTHS = (8, 5, 3)
+SIXTEENTHS = (10, 6)
 
 
 class Wires:

time: 206 us -> 168 us (0.82)
  Pallas kernels: 139 us -> 116 us
  other arithmetic: 23.2 us -> 4.17 us
  waiting for transfers between devices: 12.1 us -> 22.8 us
  starting transfers between devices: 8.78 us -> 3.37 us
    concatenate x1 -> x0, other arithmetic: 18.8 us -> none  [on_device(): rows = jnp.concatenate(stacks, axis=1)]
    pallas_call x3 -> x2, Pallas kernels: 69.4 us -> 57.3 us  [scatter_dp(): pl.pallas_call(functools.partial(scatter_kernel, ring), name='scatter%d'...]
    pallas_call x3 -> x2, Pallas kernels: 69.1 us -> 58.5 us  [gather_dp(): pl.pallas_call(functools.partial(gather_kernel, ring), name='gather%d' %...]
    ppermute x6 -> x4, waiting for transfers between devices: 8.79 us -> 15.8 us  [turn(): return lax.ppermute(block, 'expert', route)]
    ppermute x6 -> x4, starting transfers between devices: 7.51 us -> 2.82 us  [turn(): return lax.ppermute(block, 'expert', route)]
    ppermute x6 -> x4, waiting for transfers between devices: 3.31 us -> 6.92 us  [swap_cores(): return lax.ppermute(block, 'expert', [(c, c ^ 1) for c in range(col_size)])]
    dot_general x3 -> x2, matrix products: 5.42 us -> 4.79 us  [on_device(): jnp.einsum('rst,td->rsd', spots, columns[n], preferred_element_type=F32)]
  transfers between devices with their start and end apart: 12 -> 8, of which waited for: 4 -> 5; matrix products, arithmetic and copies ran while one was open for 4% -> 2% of each run, Pallas kernels for 40% -> 28%
where the time goes in v4:
time: 168 us; the launch traced here: 167 us
  Pallas kernels  116 us (69%)
  waiting for transfers between devices  22.8 us (14%)
  matrix products  15.9 us (9%)
  local copies, waits for them, and re-layouts  5.07 us (3%)
  other arithmetic  4.17 us (2%)
  starting transfers between devices  3.37 us (2%)
    pallas_call x2, Pallas kernels, gather_dp(): pl.pallas_call(functools.partial(gather_kernel, ring), name='gather%d' %...  58.5 us
    pallas_call x2, Pallas kernels, scatter_dp(): pl.pallas_call(functools.partial(scatter_kernel, ring), name='scatter%d'...  57.3 us
    ppermute x4, waiting for transfers between devices, turn(): return lax.ppermute(block, 'expert', route)  15.8 us
    ppermute x4, waiting for transfers between devices, swap_cores(): return lax.ppermute(block, 'expert', [(c, c ^ 1) for c in range(col_size)])  6.92 us
    dot_general x2, matrix products, on_device(): jnp.einsum('rst,td->rsd', spots, columns[n], preferred_element_type=F32)  4.79 us
    dot_general x2, matrix products, on_device(): jnp.einsum('rst,rsd->td', weights, home, preferred_element_type=F32)  3.75 us
  transfers between devices with their start and end apart: 8, of which 5 were waited for; matrix products, arithmetic and copies ran while one was open for 2% of the time, Pallas kernels for 28%

profile of v4, /device:TPU:0, one launch (start us, length us, event | category | flops | bytes accessed | tf_op | source)
XLA Modules:
  0.0 167.4 jit_solution(3971053970301196801)
XLA Ops:
  0.0 0.0 copy-start
  0.0 1.1 slice.71.src
  1.1 1.0 slice.72
  2.1 0.7 convert_bitcast_fusion.1
  2.7 0.7 convert_element_type.90
  3.4 0.7 convert_element_type.91
  4.1 0.1 copy.14
  4.2 0.1 copy.13
  4.4 0.1 concatenate.23.src
  4.5 37.3 %gather0.1 = bf16[1024,1408]{1,0:T(8,128)(2,1)S(1)} custom-call(bf16[128,1408]{1,0:T(8,128)(2,1)S(1)} %concatenate.23.src), custom_call_target="tpu_custom_call" | custom-call | bytes 62914560 | tf_op jit(solution)/shard_map/gather0/pallas_call | solution.py:226
  41.8 0.0 copy-start.1
  41.8 1.6 copy-done.1
  43.4 0.1 slice.95
  43.4 0.1 fusion.41
  43.6 0.1 compare_convert_fusion
  43.7 0.2 copy.15
  43.9 0.2 copy.17
  44.0 0.1 multiply_reduce_fusion.1
  44.1 0.2 fusion.24
  44.3 0.1 multiply_reduce_fusion
  44.4 0.1 convert_bitcast_fusion
  44.5 0.1 copy.28
  44.6 3.5 %convolution_convert_fusion.1 = bf16[2,256,1280]{2,1,0:T(8,128)(2,1)S(1)} fusion(bf16[1024,1408]{1,0:T(8,128)(2,1)} %copy-done.1, s32[2,1024]{1,0:T(2,128)S(1)} %bitcast.64), kind=kOutput, calls=%fused_computation.4 | convolution fusion | flops 1343356928 | bytes 3940352 | tf_op jit(solution)/shard_map/rst,td->rsd/dot_general | solution.py:346
  48.1 0.1 slice_bitcast_fusion.2
  48.2 1.6 collective-permute-start
  49.7 21.3 %gather2.1 = bf16[1024,768]{1,0:T(8,128)(2,1)S(1)} custom-call(bf16[128,768]{1,0:T(8,128)(2,1)S(1)} %slice.71.src), custom_call_target="tpu_custom_call" | custom-call | bytes 62914560 | tf_op jit(solution)/shard_map/gather2/pallas_call | solution.py:226
  71.0 1.3 fusion.8
  72.4 0.1 slice_bitcast_fusion.4
  72.4 0.5 collective-permute-start.2
  73.0 0.0 collective-permute-done
  73.0 0.1 pad_maximum_fusion
  73.1 0.1 collective-permute-start.1
  73.1 7.4 %collective-permute-done.2 = bf16[256,768]{1,0:T(8,128)(2,1)S(1)} collective-permute-done((bf16[256,768]{1,0:T(8,128)(2,1)S(1)}, bf16[256,768]{1,0:T(8,128)(2,1)S(1)}, u32[]{:S(2)}, u32[]{:S(2)}) %collective-permute-start.2) | collective-permute-done | bytes 393248 | tf_op jit(solution)/shard_map/ppermute | solution.py:273
  80.5 0.1 pad_maximum_fusion.2
  80.6 0.0 copy-start.2
  80.6 0.1 collective-permute-start.3
  80.7 2.3 %collective-permute-done.3 = bf16[512,768]{1,0:T(8,128)(2,1)S(1)} collective-permute-done((bf16[512,768]{1,0:T(8,128)(2,1)S(1)}, bf16[512,768]{1,0:T(8,128)(2,1)S(1)}, u32[]{:S(2)}, u32[]{:S(2)}) %collective-permute-start.3) | collective-permute-done | bytes 786464 | tf_op jit(solution)/shard_map/ppermute | solution.py:268
  83.0 0.0 collective-permute-done.1
  83.0 2.3 %fusion.5 = f32[1024,384]{1,0:T(8,128)S(1)} fusion(bf16[1,2048,384]{2,1,0:T(8,128)(2,1)S(1)} %copy-done, bf16[512,768]{1,0:T(8,128)(2,1)S(1)} %collective-permute-done.3, bf16[256,768]{1,0:T(8,128)(2,1)S(1)} %collective-permute-done.2, bf16[256,768]{1,0:T(8,128)(2,1)S(1)} %get-tuple-element.28, bf16[512,1280]{1,0:T(8,128)(2,1)S(1)} %collective-permute-done.1, ...), kind=kOutput, calls=%fused_computation.14 | convolution fusion | flops 1635778560 | bytes 7340032 | tf_op jit(solution)/shard_map/dot_general | solution.py:351
  85.3 0.0 copy-start.3
  85.3 2.4 %multiply_convert_fusion = bf16[1024,384]{1,0:T(8,128)(2,1)S(1)} fusion(f32[1024,384]{1,0:T(8,128)S(1)} %fusion.5, bf16[1,2048,384]{2,1,0:T(8,128)(2,1)S(1)} %copy-done.2, bf16[512,768]{1,0:T(8,128)(2,1)S(1)} %collective-permute-done.3, bf16[256,768]{1,0:T(8,128)(2,1)S(1)} %collective-permute-done.2, bf16[256,768]{1,0:T(8,128)(2,1)S(1)} %get-tuple-element.28, ...), kind=kOutput, calls=%fused_computation.18 | convolution fusion | flops 1638137856 | bytes 8126464 | tf_op jit(solution)/shard_map/dot_general | solution.py:352
  87.7 0.0 copy-done.3
  87.8 1.0 convolution_convert_fusion.2
  88.7 0.1 slice.103
  88.8 0.2 collective-permute-start.4
  89.0 2.2 %collective-permute-done.4 = bf16[512,768]{1,0:T(8,128)(2,1)S(1)} collective-permute-done((bf16[512,768]{1,0:T(8,128)(2,1)S(1)}, bf16[512,768]{1,0:T(8,128)(2,1)S(1)}, u32[]{:S(2)}, u32[]{:S(2)}) %collective-permute-start.4) | collective-permute-done | bytes 786464 | tf_op jit(solution)/shard_map/ppermute | solution.py:268
  91.1 0.2 add_convert_fusion.1
  91.4 1.5 convolution_convert_fusion
  92.9 0.1 slice.106
  93.0 0.2 collective-permute-start.5
  93.2 0.1 slice_bitcast_fusion.5
  93.2 0.3 collective-permute-start.7
  93.6 2.5 %collective-permute-done.5 = bf16[512,1280]{1,0:T(8,128)(2,1)S(1)} collective-permute-done((bf16[512,1280]{1,0:T(8,128)(2,1)S(1)}, bf16[512,1280]{1,0:T(8,128)(2,1)S(1)}, u32[]{:S(2)}, u32[]{:S(2)}) %collective-permute-start.5) | collective-permute-done | bytes 1310752 | tf_op jit(solution)/shard_map/ppermute | solution.py:268
  96.1 0.3 add_convert_fusion
  96.4 0.1 slice_bitcast_fusion
  96.5 0.3 collective-permute-start.6
  96.8 8.4 %collective-permute-done.7 = bf16[256,768]{1,0:T(8,128)(2,1)S(1)} collective-permute-done((bf16[256,768]{1,0:T(8,128)(2,1)S(1)}, bf16[256,768]{1,0:T(8,128)(2,1)S(1)}, u32[]{:S(2)}, u32[]{:S(2)}) %collective-permute-start.7) | collective-permute-done | bytes 393248 | tf_op jit(solution)/shard_map/ppermute | solution.py:273
  105.3 1.7 %bitcast_convert_fusion.1.part = bf16[1024,768]{1,0:T(8,128)(2,1)S(1)} fusion(bf16[2,1024]{1,0:T(2,128)(2,1)S(1)} %bitcast.68, s32[2,1024]{1,0:T(2,128)S(1)} %bitcast.66, bf16[1,256,768]{2,1,0:T(8,128)(2,1)S(1)} %bitcast.72, bf16[1,256,768]{2,1,0:T(8,128)(2,1)S(1)} %get-tuple-element.26), kind=kOutput, calls=%fused_computation.3 | convolution fusion | flops 807534592 | bytes 2371584 | tf_op jit(solution)/shard_map/rst,rsd->td/dot_general | solution.py:370
  107.0 25.8 %scatter1.1 = bf16[128,768]{1,0:T(8,128)(2,1)S(1)} custom-call(bf16[1024,768]{1,0:T(8,128)(2,1)S(1)} %bitcast_convert_fusion.1.part), custom_call_target="tpu_custom_call" | custom-call | bytes 62914560 | tf_op jit(solution)/shard_map/scatter1/pallas_call | solution.py:248
  132.8 0.0 collective-permute-done.6
  132.9 0.1 pad_maximum_fusion.1
  133.0 2.1 %bitcast_convert_fusion.part = bf16[1024,1280]{1,0:T(8,128)(2,1)S(1)} fusion(bf16[2,256,1280]{2,1,0:T(8,128)(2,1)S(1)} %pad_maximum_fusion.1, bf16[2,1024]{1,0:T(2,128)(2,1)S(1)} %bitcast.69, s32[2,1024]{1,0:T(2,128)S(1)} %bitcast.67), kind=kOutput, calls=%fused_computation | convolution fusion | flops 1344536576 | bytes 3944448 | tf_op jit(solution)/shard_map/rst,rsd->td/dot_general | solution.py:370
  135.0 31.4 %scatter3.1 = bf16[128,1280]{1,0:T(8,128)(2,1)S(1)} custom-call(bf16[1024,1280]{1,0:T(8,128)(2,1)S(1)} %bitcast_convert_fusion.part), custom_call_target="tpu_custom_call" | custom-call | bytes 62914560 | tf_op jit(solution)/shard_map/scatter3/pallas_call | solution.py:248
  166.5 0.8 pad_maximum_fusion.3
  (9 shorter events, 0.1 us)
Async XLA Ops:
  0.0 83.0 %copy-start = (bf16[1,2048,384]{2,1,0:T(8,128)(2,1)S(1)}, bf16[1,2048,384]{2,1,0:T(8,128)(2,1)}, u32[]{:S(2)}) copy-start(bf16[1,2048,384]{2,1,0:T(8,128)(2,1)} %param.11) | copy-start | bytes 4718596
  41.8 1.6 copy-start.1
  48.2 24.8 %collective-permute-start = (bf16[256,1280]{1,0:T(8,128)(2,1)S(1)}, bf16[256,1280]{1,0:T(8,128)(2,1)S(1)}, u32[]{:S(2)}, u32[]{:S(2)}) collective-permute-start(bf16[256,1280]{1,0:T(8,128)(2,1)S(1)} %get-tuple-element.25), channel_id=1, source_target_pairs={{0,2},{1,3},{2,0},{3,1},{4,6},{5,7},{6,4},{7,5},{8,10},{9,11},{10,... | collective-permute-start | bytes 1966088 | tf_op jit(solution)/shard_map/ppermute | solution.py:273
  72.4 8.1 %collective-permute-start.2 = (bf16[256,768]{1,0:T(8,128)(2,1)S(1)}, bf16[256,768]{1,0:T(8,128)(2,1)S(1)}, u32[]{:S(2)}, u32[]{:S(2)}) collective-permute-start(bf16[256,768]{1,0:T(8,128)(2,1)S(1)} %get-tuple-element.29), channel_id=1, source_target_pairs={{0,2},{1,3},{2,0},{3,1},{4,6},{5,7},{6,4},{7,5},{8,10},{9,11},{10,... | collective-permute-start | bytes 1179656 | tf_op jit(solution)/shard_map/ppermute | solution.py:273
  73.1 9.9 %collective-permute-start.1 = (bf16[512,1280]{1,0:T(8,128)(2,1)S(1)}, bf16[512,1280]{1,0:T(8,128)(2,1)S(1)}, u32[]{:S(2)}, u32[]{:S(2)}) collective-permute-start(bf16[512,1280]{1,0:T(8,128)(2,1)S(1)} %pad_maximum_fusion), channel_id=1, source_target_pairs={{0,1},{1,0},{2,3},{3,2},{4,5},{5,4},{6,7},{7,6},{8,9},{9,8},{10,11... | collective-permute-start | bytes 3932168 | tf_op jit(solution)/shard_map/ppermute | solution.py:268
  80.6 4.7 %copy-start.2 = (bf16[1,2048,384]{2,1,0:T(8,128)(2,1)S(1)}, bf16[1,2048,384]{2,1,0:T(8,128)(2,1)}, u32[]{:S(2)}) copy-start(bf16[1,2048,384]{2,1,0:T(8,128)(2,1)} %param.12) | copy-start | bytes 4718596
  80.6 2.4 %collective-permute-start.3 = (bf16[512,768]{1,0:T(8,128)(2,1)S(1)}, bf16[512,768]{1,0:T(8,128)(2,1)S(1)}, u32[]{:S(2)}, u32[]{:S(2)}) collective-permute-start(bf16[512,768]{1,0:T(8,128)(2,1)S(1)} %pad_maximum_fusion.2), channel_id=1, source_target_pairs={{0,1},{1,0},{2,3},{3,2},{4,5},{5,4},{6,7},{7,6},{8,9},{9,8},{10,11... | collective-permute-start | bytes 2359304 | tf_op jit(solution)/shard_map/ppermute | solution.py:268
  85.3 2.4 %copy-start.3 = (bf16[1,384,2048]{2,1,0:T(8,128)(2,1)S(1)}, bf16[1,384,2048]{2,1,0:T(8,128)(2,1)}, u32[]{:S(2)}) copy-start(bf16[1,384,2048]{2,1,0:T(8,128)(2,1)} %param.13) | copy-start | bytes 4718596
  88.8 2.4 %collective-permute-start.4 = (bf16[512,768]{1,0:T(8,128)(2,1)S(1)}, bf16[512,768]{1,0:T(8,128)(2,1)S(1)}, u32[]{:S(2)}, u32[]{:S(2)}) collective-permute-start(bf16[512,768]{1,0:T(8,128)(2,1)S(1)} %slice.103), channel_id=1, source_target_pairs={{0,1},{1,0},{2,3},{3,2},{4,5},{5,4},{6,7},{7,6},{8,9},{9,8},{10,11... | collective-permute-start | bytes 2359304 | tf_op jit(solution)/shard_map/ppermute | solution.py:268
  93.0 3.1 %collective-permute-start.5 = (bf16[512,1280]{1,0:T(8,128)(2,1)S(1)}, bf16[512,1280]{1,0:T(8,128)(2,1)S(1)}, u32[]{:S(2)}, u32[]{:S(2)}) collective-permute-start(bf16[512,1280]{1,0:T(8,128)(2,1)S(1)} %slice.106), channel_id=1, source_target_pairs={{0,1},{1,0},{2,3},{3,2},{4,5},{5,4},{6,7},{7,6},{8,9},{9,8},{10,11... | collective-permute-start | bytes 3932168 | tf_op jit(solution)/shard_map/ppermute | solution.py:268
  93.2 12.1 %collective-permute-start.7 = (bf16[256,768]{1,0:T(8,128)(2,1)S(1)}, bf16[256,768]{1,0:T(8,128)(2,1)S(1)}, u32[]{:S(2)}, u32[]{:S(2)}) collective-permute-start(bf16[256,768]{1,0:T(8,128)(2,1)S(1)} %get-tuple-element.27), channel_id=1, source_target_pairs={{0,2},{1,3},{2,0},{3,1},{4,6},{5,7},{6,4},{7,5},{8,10},{9,11},{10,... | collective-permute-start | bytes 1179656 | tf_op jit(solution)/shard_map/ppermute | solution.py:273
  96.5 36.4 %collective-permute-start.6 = (bf16[256,1280]{1,0:T(8,128)(2,1)S(1)}, bf16[256,1280]{1,0:T(8,128)(2,1)S(1)}, u32[]{:S(2)}, u32[]{:S(2)}) collective-permute-start(bf16[256,1280]{1,0:T(8,128)(2,1)S(1)} %get-tuple-element.23), channel_id=1, source_target_pairs={{0,2},{1,3},{2,0},{3,1},{4,6},{5,7},{6,4},{7,5},{8,10},{9,11},{10,... | collective-permute-start | bytes 1966088 | tf_op jit(solution)/shard_map/ppermute | solution.py:273
